TPU v7x, 256 devices: a whole 4x4x8 slice. The times are simulated.
256 devices in a mesh: sec: 8 (over y, x_lo), row: 32 (over z, x_hi, core).
Axes of the slice: x: 4 (x_hi: 2, x_lo: 2; x = x_hi * 2 + x_lo), y: 4, z: 8, core: 2. Of those that a mesh axis runs over, the one named last changes fastest.
Arguments:
- rhs: float32 [8192, 256], P(('sec', 'row')), may hold values from -6 to 6
- coupling: bfloat16 [8, 1024, 8192], P(None, 'row', 'sec'), may hold values from -0.0625 to 0.0625
- diag_inverse: bfloat16 [8, 1024, 1024], P('sec'), as said below
Outputs:
- solution: float32 [8192, 256], P(('sec', 'row'))
- forward: float32 [8192, 256], P(('sec', 'row'))
Inputs may be any that keep to these rules, and one draw needn't show every extreme that they name: `diag_inverse`: each of the 8 blocks is lower triangular with diagonal entries from 0.5 to 1.5.
All inputs are finite; a program needn't handle non-finite values.
Results may differ from a plain program's by a relative error of at most 0.02.
Values may be sent and summed in bfloat16 or wider, within the bound.
No kernel may reach another device: no remote copies, remote signals or barrier semaphores. Data moves between devices by JAX's collectives and lax.ppermute only.
A program may use at most 64 MiB of HBM per device.

v0:
```python
import functools

import jax
import jax.numpy as jnp
from jax import lax
from jax.experimental import pallas as pl
from jax.experimental.pallas import tpu as pltpu
from jax.sharding import PartitionSpec as P


BF = jnp.bfloat16
F32 = jnp.float32
SEC, ROW = 8, 32
NT = (((1,), (1,)), ((), ()))
NN = (((1,), (0,)), ((), ()))
BOTH = ("sec", "row")


def place(dev):
    sec, row = divmod(dev, ROW)
    return sec // 2, sec % 2, row // 4, (row // 2) % 2, row % 2


def device(y, xl, z, xh, core):
    return (y * 2 + xl) * ROW + z * 4 + xh * 2 + core


def moved(move):
    return [(d, device(*move(*place(d)))) for d in range(SEC * ROW)]


XL = moved(lambda y, xl, z, xh, k: (y, 1 - xl, z, xh, k))
XH = moved(lambda y, xl, z, xh, k: (y, xl, z, 1 - xh, k))
CORE = moved(lambda y, xl, z, xh, k: (y, xl, z, xh, 1 - k))
ZUP = moved(lambda y, xl, z, xh, k: (y, xl, (z + 1) % 8, xh, k))
ZDOWN = moved(lambda y, xl, z, xh, k: (y, xl, (z - 1) % 8, xh, k))
XP = moved(lambda y, xl, z, xh, k: (y, 1 - xl, z, (xh + xl) % 2, k))
XM = moved(lambda y, xl, z, xh, k: (y, 1 - xl, z, (xh + 1 - xl) % 2, k))
CROSS = moved(lambda y, xl, z, xh, k: (y, k, z, xh, xl))
YA = moved(lambda y, xl, z, xh, k: (y ^ 1, xl, z, xh, k))
YB = moved(lambda y, xl, z, xh, k: ({0: 3, 1: 2, 2: 1, 3: 0}[y], xl, z, xh, k))
PLANES = [
    [device(y, xl, z, xh, k) for xl in range(2) for xh in range(2) for z in range(8)]
    for y in range(4)
    for k in range(2)
]
RINGS = [
    [device(y, xl, z, xh, k) for z in range(8)] for y in range(4) for xl in range(2) for xh in range(2) for k in range(2)
]
SWAPS = [YA, YB, YA]


def send(x, pairs):
    return lax.ppermute(x, BOTH, pairs)


def dot(a, b, dims):
    return lax.dot_general(a, b, dims, preferred_element_type=F32)


def call(body, out, *args):
    specs = [pl.BlockSpec(memory_space=pltpu.SMEM)]
    specs += [pl.BlockSpec(memory_space=pltpu.VMEM)] * (len(args) - 1)
    many = isinstance(out, list)
    return pl.pallas_call(
        body,
        out_shape=out,
        in_specs=specs,
        out_specs=[pl.BlockSpec(memory_space=pltpu.VMEM)] * len(out) if many else pl.BlockSpec(memory_space=pltpu.VMEM),
        compiler_params=pltpu.CompilerParams(vmem_limit_bytes=20 * 2**20),
    )(*args)


def ring_z(x):
    part = x.shape[-2] // 5 * 3
    up = down = x
    ups, downs = [], []
    for _ in range(1, 4):
        up, down = send(up, ZUP), send(down, ZDOWN)
        ups.append(up)
        downs.append(down)
    last = send(up[..., :part, :], ZUP), send(down[..., part:, :], ZDOWN)
    return [x, *ups, *downs, *last]


def lay_all(ids, *refs):
    near, jump, tied = refs[-3:]
    z, x = ids[2], ids[3] * 2 + ids[1]
    part = refs[0].shape[1] // 5
    rows = 2 * part

    def spot(n, at_z):
        at_x = (x + [0, 3, 1, 2][n]) % 4
        return at_x % 2, pl.multiple_of((at_x // 2 * 8 + at_z) * rows, rows)

    for piece, offset, first in zip(refs[:9], [0, 7, 6, 5, 1, 2, 3, 4, 4], [0] * 8 + [3]):
        for n in range(4):
            xl, start = spot(n, (z + offset) % 8)
            for block in range(piece.shape[1] // part):
                number = first + block
                rows_in = slice(block * part, (block + 1) * part)
                if number < 4:
                    begin = pl.multiple_of(start + number % 2 * part, part)
                    near[number // 2, xl, pl.ds(begin, part)] = piece[n, rows_in]
                else:
                    tied[pl.ds(pl.multiple_of(start + xl * part, part), part)] = piece[n, rows_in]
    for n, plane in enumerate(refs[9:13]):
        for at_z in range(8):
            xl, start = spot(n, at_z)
            jump[xl, pl.ds(start, rows)] = plane[at_z]


def lay_tied(ids, own, other, out):
    half = own.shape[0]
    out[pl.ds(pl.multiple_of(ids[4] * half, half), half)] = own[...]
    out[pl.ds(pl.multiple_of((1 - ids[4]) * half, half), half)] = other[...]


def wide(core, own, other, s, half):
    a, b = own[:, s * half : (s + 1) * half], other[:, s * half : (s + 1) * half]
    low = jnp.where(core == 0, a, b)
    high = jnp.where(core == 0, b, a)
    return jnp.concatenate([low, high], axis=1)


def forward_body(stage, ids, own, other, old, near, jump, tied, near_from, jump_from, *outs):
    y, core = ids[0], ids[4]
    half = own.shape[1] // 2
    width = 2 * half
    top = wide(core, own[...], other[...], 0, half).astype(BF)
    bottom = wide(core, own[...], other[...], 1, half) - dot(top, tied[...], NT)
    new = jnp.concatenate([top, bottom.astype(BF)], axis=1)
    kept = jnp.where(y == stage, new, old[...])
    outs[0][...] = kept
    if stage == 3:
        return
    source = kept if stage < 2 else jnp.where(y == 3, near_from[...], kept)
    for t in range(2):
        total = dot(source[:, :width], near[t, 0], NT) + dot(source[:, width:], near[t, 1], NT)
        outs[1][:, t * half : (t + 1) * half] = total
    source = kept if stage == 0 else jump_from[...]
    outs[1][:, width:] = dot(source[:, :width], jump[0], NT) + dot(source[:, width:], jump[1], NT)


def products_body(ids, near_from, jump_from, near, jump, by_near, by_jump):
    half = near_from.shape[1] // 2
    width = 2 * half
    a, b = near_from[:, :half], near_from[:, half:]

    def column(c, carry):
        at = pl.ds(pl.multiple_of(c * width, width), width)
        by_near[:, at] = dot(a, near[0, c], NN) + dot(b, near[1, c], NN)
        by_jump[:, at] = dot(jump_from[...], jump[c], NN)
        return carry

    lax.fori_loop(0, 2, column, 0)


def solve_body(stage, ids, back, own, other, old, tied, jump, *outs):
    y, core = ids[0], ids[4]
    width = back.shape[1] // 2
    half = width // 2
    u = back[...] - (own[...].astype(F32) + other[...].astype(F32))
    x1 = u[:, width:]
    x0 = u[:, :width] - dot(x1.astype(BF), tied[...], NN)
    kept = jnp.where(y == 3 - stage, jnp.concatenate([x0, x1], axis=1), old[...])
    outs[0][...] = kept
    if stage == 3:
        return
    parts = [
        jnp.where(core == 0, kept[:, s * width : s * width + half], kept[:, s * width + half : (s + 1) * width])
        for s in range(2)
    ]
    outs[1][...] = jnp.concatenate(parts, axis=1).astype(BF)
    if stage == 0:
        for c in range(2):
            outs[2][:, c * width : (c + 1) * width] = dot(parts[1].astype(BF), jump[c], NN)


def solve(rhs, coupling, diag_inverse):
    sec = lax.axis_index("sec")
    row = lax.axis_index("row")
    y, xl = sec // 2, sec % 2
    z, xh, core = row // 4, (row // 2) % 2, row % 2
    ids = jnp.stack([y, xl, z, xh, core]).astype(jnp.int32)
    rows, total = rhs.shape
    width = diag_inverse.shape[1]
    half = width // 2
    cols = total // ROW

    slot = jnp.arange(width)
    i, rest = slot % rows, slot // rows
    natural = ((rest % 8) * 4 + ((rest // 8) % 2) * 2 + rest // 16) * rows + i
    pick = (jnp.arange(width)[:, None] == natural[None, :]).astype(BF)
    inverse = dot(diag_inverse[0], pick, NN).astype(BF)
    m = dot(coupling.reshape(SEC * rows, width), inverse, NN).astype(BF)
    m = m.reshape(SEC, rows, width)

    def blocks(first, count):
        return lax.dynamic_slice_in_dim(m, first, count, 0)

    far = send(m[6:8], YB)
    close = lax.ppermute(blocks(5 + 2 * (y % 2), 1), "sec", [(0, 2), (1, 3), (2, 6), (3, 7)])
    inner = blocks(2 * y + 1, 1)[0]
    given = send(inner[rows // 2 :], XL)
    next_pair = jnp.where(y == 3, far, blocks(jnp.minimum(2 * y + 2, 6), 2))
    skip = jnp.where(y == 0, m[4], jnp.where(y == 2, far[0], close[0]))
    inner = jnp.where(xl == 0, inner[: rows // 2], given)

    lanes = rhs.T.reshape(8, 2, 2, cols, rows).transpose(2, 1, 0, 3, 4).reshape(ROW, cols * rows // 128, 128)
    mine = lax.all_to_all(lanes, BOTH, 0, 0, axis_index_groups=PLANES, tiled=True)
    mine = mine.reshape(2, 16, cols, rows).transpose(2, 0, 1, 3).reshape(cols, width)

    unit = jnp.concatenate([next_pair.reshape(2 * rows, width), inner], axis=0)
    unit = jnp.stack([unit, send(unit, XP), send(unit, XM), send(unit, XH)])
    plane = lax.all_to_all(jnp.broadcast_to(skip, (8, rows, width)), BOTH, 0, 0, axis_index_groups=RINGS, tiled=True)
    planes = [plane, send(plane, XP), send(plane, XM), send(plane, XH)]
    pieces = ring_z(unit) + planes
    pieces = [pltpu.with_memory_space_constraint(p, pltpu.VMEM) for p in pieces]
    shapes = [pltpu.VMEM((2, 2, half, width), BF), pltpu.VMEM((2, half, width), BF), pltpu.VMEM((half, width), BF)]
    away = send(inverse, [(a, b) for a, b in CROSS if a != b])
    inverse = jnp.where(core == xl, inverse, away)
    early = jnp.where(core == 0, jnp.ones((8, 128), F32), 0.0)
    near, jump, tied = call(lay_all, shapes, ids, *pieces, mine, inverse, early)
    tied = call(lay_tied, pltpu.VMEM((width, width), BF), ids, tied, send(tied, CORE))

    def struct(n, dtype):
        return jax.ShapeDtypeStruct((cols, n), dtype)

    zero_z = jnp.zeros((cols, 2 * width), BF)
    kept, got_z, resid, stash, ours = zero_z, zero_z, mine, None, None
    for stage in range(4):
        shapes = [struct(2 * width, BF)] + ([struct(width + half, F32)] if stage < 3 else [])
        got = call(
            functools.partial(forward_body, stage), shapes, ids, resid, send(resid, CORE), kept, near, jump, tied, got_z, got_z
        )
        kept = got[0]
        if stage == 3:
            break
        update, leap = got[1][:, :width], got[1][:, width:]
        if stage == 0:
            sent = jnp.concatenate([update.astype(BF), leap.astype(BF), kept], axis=1)
        elif stage == 1:
            update = update + jnp.concatenate([stash.astype(F32), leap], axis=1)
            sent = jnp.concatenate([update.astype(BF), kept], axis=1)
        else:
            ours = update
            update = update + jnp.concatenate([leap, jnp.zeros_like(leap)], axis=1)
            sent = jnp.concatenate([update.astype(BF), got_z], axis=1)
        arrived = send(sent, SWAPS[stage])
        acc, got_z = arrived[:, :width].astype(F32), arrived[:, -2 * width :]
        if stage == 0:
            stash = arrived[:, width : width + half]
        if stage == 2:
            late = dot(got_z[:, :width], jump[0], NT) + dot(got_z[:, width:], jump[1], NT)
            acc = acc + ours + jnp.concatenate([jnp.zeros_like(late), late], axis=1)
        resid = mine - acc

    def mine_of(pair):
        return jnp.where(core == 0, pair[:, :width], pair[:, width:])

    solved = dot(mine_of(kept), inverse, NT)
    back = dot(solved.astype(BF), inverse, NN)
    other = send(back, CORE)
    back = jnp.concatenate([jnp.where(core == 0, back, other), jnp.where(core == 0, other, back)], axis=1)

    zero = jnp.zeros((cols, 2 * width), F32)
    answer, halves, own, other = zero, None, zero.astype(BF), zero.astype(BF)
    arrived, ours = None, None
    for stage in range(4):
        if stage > 0:
            got_x = arrived[:, :width]
            got_c = arrived[:, width : 3 * width].astype(F32)
            if stage == 1:
                sources = jnp.where(y == 3, halves, got_x), got_x[:, :half]
            elif stage == 2:
                sources = got_x, got_x[:, half:]
            else:
                sources = got_x, arrived[:, 3 * width :]
            by_near, by_jump = call(products_body, [struct(2 * width, F32)] * 2, ids, *sources, near, jump)
            if stage == 1:
                own = by_near
                give = jnp.where(y == 3, by_near, by_jump + got_c)
            elif stage == 2:
                own, ours, give = by_near + got_c, got_c, by_jump
            else:
                own = by_near + by_jump + got_c + ours
            own = own.astype(BF)
            other = send(own, CORE)
        shapes = [struct(2 * width, F32)]
        shapes += [struct(width, BF)] if stage < 3 else []
        shapes += [struct(2 * width, F32)] if stage == 0 else []
        got = call(functools.partial(solve_body, stage), shapes, ids, back, own, other, answer, tied, jump)
        answer = got[0]
        if stage == 3:
            break
        halves = got[1]
        if stage == 0:
            give = got[2]
        sent = [halves, give.astype(BF)] + ([got_x[:, :half]] if stage == 2 else [])
        arrived = send(jnp.concatenate(sent, axis=1), SWAPS[stage])

    final = send(jnp.concatenate([mine_of(answer), solved], axis=1).astype(BF), CROSS)
    solved = final[:, width:].reshape(cols, ROW, rows).transpose(1, 0, 2)
    final = final[:, :width].reshape(cols, 2, 2, 8, rows).transpose(3, 2, 1, 0, 4).reshape(ROW, cols, rows)
    final = jnp.concatenate([final, solved], axis=1).reshape(ROW, 2 * cols * rows // 128, 128)
    got = lax.all_to_all(final, "row", 0, 0, tiled=True).astype(F32)
    got = got.reshape(ROW, 2, cols, rows).transpose(1, 3, 0, 2).reshape(2, rows, total)
    return (got[0], got[1])


def solution(mesh):
    return jax.shard_map(
        solve,
        mesh=mesh,
        in_specs=(P(("sec", "row"), None), P(None, "row", "sec"), P("sec", None, None)),
        out_specs=(P(("sec", "row"), None), P(("sec", "row"), None)),
        check_vma=False,
    )
```

profile of v0, /device:TPU:4, one launch (start us, length us, event | category | flops | bytes accessed | tf_op | source)
XLA Modules:
  0.0 200.5 jit_solution(15708118699231466155)
XLA Ops:
  2.2 3.7 %fusion.3 = bf16[1024,1024]{0,1:T(8,128)(2,1)} fusion(bf16[1,1024,1024]{2,1,0:T(8,128)(2,1)S(1)} %copy-done, s32[1024]{0:T(1024)S(1)} %fusion.32), kind=kOutput, calls=%fused_computation.5 | convolution fusion | flops 2149580800 | bytes 4198400 | tf_op jit(solution)/shard_map/dot_general | solution.py:58
  6.0 2.3 %convolution_convert_fusion = bf16[1024,256]{0,1:T(8,128)(2,1)S(1)} fusion(bf16[256,1024]{1,0:T(8,128)(2,1)S(1)} %bitcast.81, bf16[1024,1024]{0,1:T(8,128)(2,1)} %fusion.3), kind=kOutput, calls=%fused_computation.6 | convolution fusion | flops 537133056 | bytes 3145728 | tf_op jit(solution)/shard_map/dot_general | solution.py:58
  9.6 3.1 %collective-permute-start.1 = (bf16[2,32,1024]{2,1,0:T(8,128)(2,1)S(1)}, bf16[2,32,1024]{2,1,0:T(8,128)(2,1)S(1)}, u32[]{:S(2)}, u32[]{:S(2)}) collective-permute-start(bf16[2,32,1024]{2,1,0:T(8,128)(2,1)S(1)} %bitcast.80), channel_id=1, source_target_pairs={{0,192},{1,193},{2,194},{3,195},{4,196},{5,197},{6,198},{7,199},{8... | collective-permute-start | bytes 393224 | tf_op jit(solution)/shard_map/ppermute | solution.py:54
  12.7 3.2 %collective-permute-done.1 = bf16[2,32,1024]{2,1,0:T(8,128)(2,1)S(1)} collective-permute-done((bf16[2,32,1024]{2,1,0:T(8,128)(2,1)S(1)}, bf16[2,32,1024]{2,1,0:T(8,128)(2,1)S(1)}, u32[]{:S(2)}, u32[]{:S(2)}) %collective-permute-start.1) | collective-permute-done | bytes 131104 | tf_op jit(solution)/shard_map/ppermute | solution.py:54
  18.1 2.2 %collective-permute-start.5 = (bf16[80,1024]{1,0:T(8,128)(2,1)S(1)}, bf16[80,1024]{1,0:T(8,128)(2,1)S(1)}, u32[]{:S(2)}, u32[]{:S(2)}) collective-permute-start(bf16[80,1024]{1,0:T(8,128)(2,1)S(1)} %get-tuple-element.51), channel_id=1, source_target_pairs={{0,2},{1,3},{2,0},{3,1},{4,6},{5,7},{6,4},{7,5},{8,10},{9,11},{10,... | collective-permute-start | bytes 491528 | tf_op jit(solution)/shard_map/ppermute | solution.py:54
  20.3 2.3 %collective-permute-done.3 = bf16[80,1024]{1,0:T(8,128)(2,1)S(1)} collective-permute-done((bf16[80,1024]{1,0:T(8,128)(2,1)S(1)}, bf16[80,1024]{1,0:T(8,128)(2,1)S(1)}, u32[]{:S(2)}, u32[]{:S(2)}) %collective-permute-start.3) | collective-permute-done | bytes 163872 | tf_op jit(solution)/shard_map/ppermute | solution.py:54
  23.2 2.4 %collective-permute-done.5 = bf16[80,1024]{1,0:T(8,128)(2,1)S(1)} collective-permute-done((bf16[80,1024]{1,0:T(8,128)(2,1)S(1)}, bf16[80,1024]{1,0:T(8,128)(2,1)S(1)}, u32[]{:S(2)}, u32[]{:S(2)}) %collective-permute-start.5) | collective-permute-done | bytes 163872 | tf_op jit(solution)/shard_map/ppermute | solution.py:54
  29.0 4.0 %collective-permute-start.9 = (bf16[4,80,1024]{2,1,0:T(8,128)(2,1)S(1)}, bf16[4,80,1024]{2,1,0:T(8,128)(2,1)}, u32[]{:S(2)}, u32[]{:S(2)}) collective-permute-start(bf16[4,80,1024]{2,1,0:T(8,128)(2,1)S(1)} %pad_maximum_fusion.refs_0_), channel_id=1, source_target_pairs={{0,28},{1,29},{2,30},{3,31},{4,0},{5,1},{6,2},{7,3},{8,4},{9,5},{1... | collective-permute-start | bytes 1966088 | tf_op jit(solution)/shard_map/ppermute | solution.py:54
  33.0 10.4 %collective-permute-done.6.refs_1_ = bf16[4,80,1024]{2,1,0:T(8,128)(2,1)} collective-permute-done((bf16[4,80,1024]{2,1,0:T(8,128)(2,1)S(1)}, bf16[4,80,1024]{2,1,0:T(8,128)(2,1)}, u32[]{:S(2)}, u32[]{:S(2)}) %collective-permute-start.6) | collective-permute-done | bytes 655392 | tf_op jit(solution)/shard_map/ppermute | solution.py:54
  43.4 2.2 %collective-permute-start.14 = (bf16[1,32,1024]{2,1,0:T(8,128)(2,1)S(1)}, bf16[1,32,1024]{2,1,0:T(8,128)(2,1)S(1)}, u32[]{:S(2)}, u32[]{:S(2)}) collective-permute-start(bf16[1,32,1024]{2,1,0:T(8,128)(2,1)S(1)} %constant_dynamic-slice_fusion), channel_id=1, source_target_pairs={{0,64},{32,96},{64,192},{96,224},{1,65},{33,97},{65,193},{97,225},... | collective-permute-start | bytes 196616 | tf_op jit(solution)/shard_map/ppermute | solution.py:203
  46.6 3.8 %collective-permute-start.10 = (bf16[4,80,1024]{2,1,0:T(8,128)(2,1)}, bf16[4,80,1024]{2,1,0:T(8,128)(2,1)}, u32[]{:S(2)}, u32[]{:S(2)}) collective-permute-start(bf16[4,80,1024]{2,1,0:T(8,128)(2,1)} %collective-permute-done.9.refs_4_), channel_id=1, source_target_pairs={{0,28},{1,29},{2,30},{3,31},{4,0},{5,1},{6,2},{7,3},{8,4},{9,5},{1... | collective-permute-start | bytes 1966088 | tf_op jit(solution)/shard_map/ppermute | solution.py:54
  51.3 5.8 %all-to-all-start.1 = ((bf16[8,32,1024]{2,1,0:T(8,128)(2,1)}), bf16[8,32,1024]{2,1,0:T(8,128)(2,1)S(1)}, u32[]{:S(2)}, u32[]{:S(2)}) async-start(bf16[8,32,1024]{2,1,0:T(8,128)(2,1)} %broadcast_in_dim.5), calls=%async_computation.1 | async-start | bytes 1048576 | tf_op jit(solution)/shard_map/all_to_all | solution.py:216
  59.1 6.5 %collective-permute-done.10.refs_5_ = bf16[4,80,1024]{2,1,0:T(8,128)(2,1)} collective-permute-done((bf16[4,80,1024]{2,1,0:T(8,128)(2,1)}, bf16[4,80,1024]{2,1,0:T(8,128)(2,1)}, u32[]{:S(2)}, u32[]{:S(2)}) %collective-permute-start.10) | collective-permute-done | bytes 655392 | tf_op jit(solution)/shard_map/ppermute | solution.py:54
  65.6 3.9 %collective-permute-start.11 = (bf16[4,80,1024]{2,1,0:T(8,128)(2,1)}, bf16[4,80,1024]{2,1,0:T(8,128)(2,1)}, u32[]{:S(2)}, u32[]{:S(2)}) collective-permute-start(bf16[4,80,1024]{2,1,0:T(8,128)(2,1)} %collective-permute-done.10.refs_5_), channel_id=1, source_target_pairs={{0,28},{1,29},{2,30},{3,31},{4,0},{5,1},{6,2},{7,3},{8,4},{9,5},{1... | collective-permute-start | bytes 1966088 | tf_op jit(solution)/shard_map/ppermute | solution.py:54
  69.5 7.0 %all-to-all-done.1.refs_9_ = bf16[8,32,1024]{2,1,0:T(8,128)(2,1)S(1)} async-done(((bf16[8,32,1024]{2,1,0:T(8,128)(2,1)}), bf16[8,32,1024]{2,1,0:T(8,128)(2,1)S(1)}, u32[]{:S(2)}, u32[]{:S(2)}) %all-to-all-start.1) | async-done | bytes 524320 | tf_op jit(solution)/shard_map/all_to_all | solution.py:216
  78.5 8.8 %collective-permute-done.8.refs_3_ = bf16[4,80,1024]{2,1,0:T(8,128)(2,1)} collective-permute-done((bf16[4,80,1024]{2,1,0:T(8,128)(2,1)}, bf16[4,80,1024]{2,1,0:T(8,128)(2,1)}, u32[]{:S(2)}, u32[]{:S(2)}) %collective-permute-start.8) | collective-permute-done | bytes 655392 | tf_op jit(solution)/shard_map/ppermute | solution.py:54
  91.1 7.7 %all-to-all-start = ((f32[32,2,128]{2,1,0:T(2,128)}), f32[32,2,128]{2,1,0:T(2,128)S(1)}, u32[]{:S(2)}, u32[]{:S(2)}) async-start(f32[32,2,128]{2,1,0:T(2,128)} %reshape.127), calls=%async_computation | async-start | bytes 65536 | tf_op jit(solution)/shard_map/all_to_all | solution.py:211
  102.1 4.6 %all-to-all-done = f32[32,2,128]{2,1,0:T(2,128)S(1)} async-done(((f32[32,2,128]{2,1,0:T(2,128)}), f32[32,2,128]{2,1,0:T(2,128)S(1)}, u32[]{:S(2)}, u32[]{:S(2)}) %all-to-all-start) | async-done | bytes 32800 | tf_op jit(solution)/shard_map/all_to_all | solution.py:211
  110.3 5.5 %collective-permute-done.13.refs_8_ = bf16[4,32,1024]{2,1,0:T(8,128)(2,1)S(1)} collective-permute-done((bf16[4,32,1024]{2,1,0:T(8,128)(2,1)S(1)}, bf16[4,32,1024]{2,1,0:T(8,128)(2,1)S(1)}, u32[]{:S(2)}, u32[]{:S(2)}) %collective-permute-start.13) | collective-permute-done | bytes 262176 | tf_op jit(solution)/shard_map/ppermute | solution.py:54
  115.8 3.2 %shard_map.50 = (bf16[2,2,512,1024]{3,2,1,0:T(8,128)(2,1)S(1)}, bf16[2,512,1024]{2,1,0:T(8,128)(2,1)S(1)}, bf16[512,1024]{1,0:T(8,128)(2,1)S(1)}) custom-call(s32[5]{0:T(128)S(1)} %stack.38.ids, bf16[4,80,1024]{2,1,0:T(8,128)(2,1)S(1)} %pad_maximum_fusion.refs_0_, bf16[4,80,1024]{2,1,0:T(8,128)(2,1)} %collective-permute-done.6.refs_1_, ...), custom_call_target="tpu_custom_call" | custom-call | tf_op jit(solution)/shard_map/pallas_call | solution.py:65
  122.5 2.8 %shard_map.52 = (bf16[8,2048]{1,0:T(8,128)(2,1)S(1)}, f32[8,1536]{1,0:T(8,128)S(1)}) custom-call(s32[5]{0:T(128)S(1)} %stack.38.ids, f32[8,1024]{1,0:T(8,128)S(1)} %reshape.129.refs_13_.own, f32[8,1024]{1,0:T(8,128)S(1)} %collective-permute-done.other, bf16[8,2048]{1,0:T(8,128)(2,1)S(1)} %broadcast_5_old_near_from_jump_from_own_other.2.old.near_from.jump_from.own.other, ...), custom_call_target="tpu_custom_call" | custom-call | tf_op jit(solution)/shard_map/pallas_call | solution.py:65
  125.4 4.2 %collective-permute-done.20 = bf16[8,3584]{1,0:T(8,128)(2,1)S(1)} collective-permute-done((bf16[8,3584]{1,0:T(8,128)(2,1)S(1)}, bf16[8,3584]{1,0:T(8,128)(2,1)S(1)}, u32[]{:S(2)}, u32[]{:S(2)}) %collective-permute-start.20) | collective-permute-done | bytes 57376 | tf_op jit(solution)/shard_map/ppermute | solution.py:54
  130.8 2.8 %shard_map.53 = (bf16[8,2048]{1,0:T(8,128)(2,1)S(1)}, f32[8,1536]{1,0:T(8,128)S(1)}) custom-call(s32[5]{0:T(128)S(1)} %stack.38.ids, f32[8,1024]{1,0:T(8,128)S(1)} %convert_subtract_fusion.1.own, f32[8,1024]{1,0:T(8,128)S(1)} %collective-permute-done.21.other, bf16[8,2048]{1,0:T(8,128)(2,1)S(1)} %get-tuple-element.28.old, ...), custom_call_target="tpu_custom_call" | custom-call | tf_op jit(solution)/shard_map/pallas_call | solution.py:65
  133.7 2.8 %collective-permute-start.22 = (bf16[8,3072]{1,0:T(8,128)(2,1)S(1)}, bf16[8,3072]{1,0:T(8,128)(2,1)S(1)}, u32[]{:S(2)}, u32[]{:S(2)}) collective-permute-start(bf16[8,3072]{1,0:T(8,128)(2,1)S(1)} %pad_maximum_fusion.6), channel_id=1, source_target_pairs={{0,192},{1,193},{2,194},{3,195},{4,196},{5,197},{6,198},{7,199},{8... | collective-permute-start | bytes 147464 | tf_op jit(solution)/shard_map/ppermute | solution.py:54
  136.4 2.6 %collective-permute-done.22 = bf16[8,3072]{1,0:T(8,128)(2,1)S(1)} collective-permute-done((bf16[8,3072]{1,0:T(8,128)(2,1)S(1)}, bf16[8,3072]{1,0:T(8,128)(2,1)S(1)}, u32[]{:S(2)}, u32[]{:S(2)}) %collective-permute-start.22) | collective-permute-done | bytes 49184 | tf_op jit(solution)/shard_map/ppermute | solution.py:54
  140.3 2.8 %shard_map.54 = (bf16[8,2048]{1,0:T(8,128)(2,1)S(1)}, f32[8,1536]{1,0:T(8,128)S(1)}) custom-call(s32[5]{0:T(128)S(1)} %stack.38.ids, f32[8,1024]{1,0:T(8,128)S(1)} %convert_subtract_fusion.own, f32[8,1024]{1,0:T(8,128)S(1)} %collective-permute-done.23.other, bf16[8,2048]{1,0:T(8,128)(2,1)S(1)} %get-tuple-element.30.old, ...), custom_call_target="tpu_custom_call" | custom-call | tf_op jit(solution)/shard_map/pallas_call | solution.py:65
  143.2 4.1 %collective-permute-done.24 = bf16[8,3072]{1,0:T(8,128)(2,1)S(1)} collective-permute-done((bf16[8,3072]{1,0:T(8,128)(2,1)S(1)}, bf16[8,3072]{1,0:T(8,128)(2,1)S(1)}, u32[]{:S(2)}, u32[]{:S(2)}) %collective-permute-start.24) | collective-permute-done | bytes 49184 | tf_op jit(solution)/shard_map/ppermute | solution.py:54
  154.2 4.1 %collective-permute-done.27 = bf16[8,3072]{1,0:T(8,128)(2,1)S(1)} collective-permute-done((bf16[8,3072]{1,0:T(8,128)(2,1)S(1)}, bf16[8,3072]{1,0:T(8,128)(2,1)S(1)}, u32[]{:S(2)}, u32[]{:S(2)}) %collective-permute-start.27) | collective-permute-done | bytes 49184 | tf_op jit(solution)/shard_map/ppermute | solution.py:54
  162.1 2.8 %collective-permute-start.29 = (bf16[8,3072]{1,0:T(8,128)(2,1)S(1)}, bf16[8,3072]{1,0:T(8,128)(2,1)S(1)}, u32[]{:S(2)}, u32[]{:S(2)}) collective-permute-start(bf16[8,3072]{1,0:T(8,128)(2,1)S(1)} %pad_maximum_fusion.9), channel_id=1, source_target_pairs={{0,192},{1,193},{2,194},{3,195},{4,196},{5,197},{6,198},{7,199},{8... | collective-permute-start | bytes 147464 | tf_op jit(solution)/shard_map/ppermute | solution.py:54
  164.8 2.6 %collective-permute-done.29 = bf16[8,3072]{1,0:T(8,128)(2,1)S(1)} collective-permute-done((bf16[8,3072]{1,0:T(8,128)(2,1)S(1)}, bf16[8,3072]{1,0:T(8,128)(2,1)S(1)}, u32[]{:S(2)}, u32[]{:S(2)}) %collective-permute-start.29) | collective-permute-done | bytes 49184 | tf_op jit(solution)/shard_map/ppermute | solution.py:54
  171.4 4.2 %collective-permute-done.31 = bf16[8,3584]{1,0:T(8,128)(2,1)S(1)} collective-permute-done((bf16[8,3584]{1,0:T(8,128)(2,1)S(1)}, bf16[8,3584]{1,0:T(8,128)(2,1)S(1)}, u32[]{:S(2)}, u32[]{:S(2)}) %collective-permute-start.31) | collective-permute-done | bytes 57376 | tf_op jit(solution)/shard_map/ppermute | solution.py:54
  180.6 18.4 %all_to_all.15 = bf16[32,4,128]{2,1,0:T(4,128)(2,1)S(1)} all-to-all(bf16[32,4,128]{2,1,0:T(4,128)(2,1)S(1)} %reshape.136), channel_id=1, replica_groups=mesh['sec'=8,'row'=32] {'row'}, dimensions={0} | all-to-all | bytes 65536 | tf_op jit(solution)/shard_map/all_to_all | solution.py:307
  (132 shorter events, 52.6 us)
Async XLA Ops:
  8.3 4.4 %collective-permute-start.2 = (bf16[16,1024]{1,0:T(8,128)(2,1)S(1)}, bf16[16,1024]{1,0:T(8,128)(2,1)S(1)}, u32[]{:S(2)}, u32[]{:S(2)}) collective-permute-start(bf16[16,1024]{1,0:T(8,128)(2,1)S(1)} %dynamic-slice_bitcast_fusion), channel_id=1, source_target_pairs={{0,32},{1,33},{2,34},{3,35},{4,36},{5,37},{6,38},{7,39},{8,40},{9,... | collective-permute-start | bytes 98312 | tf_op jit(solution)/shard_map/ppermute | solution.py:54
  9.6 6.3 %collective-permute-start.1 = (bf16[2,32,1024]{2,1,0:T(8,128)(2,1)S(1)}, bf16[2,32,1024]{2,1,0:T(8,128)(2,1)S(1)}, u32[]{:S(2)}, u32[]{:S(2)}) collective-permute-start(bf16[2,32,1024]{2,1,0:T(8,128)(2,1)S(1)} %bitcast.80), channel_id=1, source_target_pairs={{0,192},{1,193},{2,194},{3,195},{4,196},{5,197},{6,198},{7,199},{8... | collective-permute-start | bytes 393224 | tf_op jit(solution)/shard_map/ppermute | solution.py:54
  16.0 6.6 %collective-permute-start.3 = (bf16[80,1024]{1,0:T(8,128)(2,1)S(1)}, bf16[80,1024]{1,0:T(8,128)(2,1)S(1)}, u32[]{:S(2)}, u32[]{:S(2)}) collective-permute-start(bf16[80,1024]{1,0:T(8,128)(2,1)S(1)} %get-tuple-element.51), channel_id=1, source_target_pairs={{0,32},{1,33},{2,34},{3,35},{4,36},{5,37},{6,38},{7,39},{8,40},{9,... | collective-permute-start | bytes 491528 | tf_op jit(solution)/shard_map/ppermute | solution.py:54
  16.9 6.3 %collective-permute-start.4 = (bf16[80,1024]{1,0:T(8,128)(2,1)S(1)}, bf16[80,1024]{1,0:T(8,128)(2,1)S(1)}, u32[]{:S(2)}, u32[]{:S(2)}) collective-permute-start(bf16[80,1024]{1,0:T(8,128)(2,1)S(1)} %get-tuple-element.51), channel_id=1, source_target_pairs={{0,34},{1,35},{2,32},{3,33},{4,38},{5,39},{6,36},{7,37},{8,42},{9,... | collective-permute-start | bytes 491528 | tf_op jit(solution)/shard_map/ppermute | solution.py:54
  18.1 7.6 %collective-permute-start.5 = (bf16[80,1024]{1,0:T(8,128)(2,1)S(1)}, bf16[80,1024]{1,0:T(8,128)(2,1)S(1)}, u32[]{:S(2)}, u32[]{:S(2)}) collective-permute-start(bf16[80,1024]{1,0:T(8,128)(2,1)S(1)} %get-tuple-element.51), channel_id=1, source_target_pairs={{0,2},{1,3},{2,0},{3,1},{4,6},{5,7},{6,4},{7,5},{8,10},{9,11},{10,... | collective-permute-start | bytes 491528 | tf_op jit(solution)/shard_map/ppermute | solution.py:54
  25.7 17.7 %collective-permute-start.6 = (bf16[4,80,1024]{2,1,0:T(8,128)(2,1)S(1)}, bf16[4,80,1024]{2,1,0:T(8,128)(2,1)}, u32[]{:S(2)}, u32[]{:S(2)}) collective-permute-start(bf16[4,80,1024]{2,1,0:T(8,128)(2,1)S(1)} %pad_maximum_fusion.refs_0_), channel_id=1, source_target_pairs={{0,4},{1,5},{2,6},{3,7},{4,8},{5,9},{6,10},{7,11},{8,12},{9,13},{1... | collective-permute-start | bytes 1966088 | tf_op jit(solution)/shard_map/ppermute | solution.py:54
  27.0 80.9 %collective-permute-start.18 = (bf16[1024,1024]{1,0:T(8,128)(2,1)}, bf16[1024,1024]{1,0:T(8,128)(2,1)}, u32[]{:S(2)}, u32[]{:S(2)}) collective-permute-start(bf16[1024,1024]{1,0:T(8,128)(2,1)} %bitcast.23), channel_id=1, source_target_pairs={{1,32},{3,34},{5,36},{7,38},{9,40},{11,42},{13,44},{15,46},{17,48}... | collective-permute-start | bytes 6291464 | tf_op jit(solution)/shard_map/ppermute | solution.py:54
  29.0 17.5 %collective-permute-start.9 = (bf16[4,80,1024]{2,1,0:T(8,128)(2,1)S(1)}, bf16[4,80,1024]{2,1,0:T(8,128)(2,1)}, u32[]{:S(2)}, u32[]{:S(2)}) collective-permute-start(bf16[4,80,1024]{2,1,0:T(8,128)(2,1)S(1)} %pad_maximum_fusion.refs_0_), channel_id=1, source_target_pairs={{0,28},{1,29},{2,30},{3,31},{4,0},{5,1},{6,2},{7,3},{8,4},{9,5},{1... | collective-permute-start | bytes 1966088 | tf_op jit(solution)/shard_map/ppermute | solution.py:54
  43.4 15.1 %collective-permute-start.7 = (bf16[4,80,1024]{2,1,0:T(8,128)(2,1)}, bf16[4,80,1024]{2,1,0:T(8,128)(2,1)}, u32[]{:S(2)}, u32[]{:S(2)}) collective-permute-start(bf16[4,80,1024]{2,1,0:T(8,128)(2,1)} %collective-permute-done.6.refs_1_), channel_id=1, source_target_pairs={{0,4},{1,5},{2,6},{3,7},{4,8},{5,9},{6,10},{7,11},{8,12},{9,13},{1... | collective-permute-start | bytes 1966088 | tf_op jit(solution)/shard_map/ppermute | solution.py:54
  43.4 6.9 %collective-permute-start.14 = (bf16[1,32,1024]{2,1,0:T(8,128)(2,1)S(1)}, bf16[1,32,1024]{2,1,0:T(8,128)(2,1)S(1)}, u32[]{:S(2)}, u32[]{:S(2)}) collective-permute-start(bf16[1,32,1024]{2,1,0:T(8,128)(2,1)S(1)} %constant_dynamic-slice_fusion), channel_id=1, source_target_pairs={{0,64},{32,96},{64,192},{96,224},{1,65},{33,97},{65,193},{97,225},... | collective-permute-start | bytes 196616 | tf_op jit(solution)/shard_map/ppermute | solution.py:203
  46.6 19.0 %collective-permute-start.10 = (bf16[4,80,1024]{2,1,0:T(8,128)(2,1)}, bf16[4,80,1024]{2,1,0:T(8,128)(2,1)}, u32[]{:S(2)}, u32[]{:S(2)}) collective-permute-start(bf16[4,80,1024]{2,1,0:T(8,128)(2,1)} %collective-permute-done.9.refs_4_), channel_id=1, source_target_pairs={{0,28},{1,29},{2,30},{3,31},{4,0},{5,1},{6,2},{7,3},{8,4},{9,5},{1... | collective-permute-start | bytes 1966088 | tf_op jit(solution)/shard_map/ppermute | solution.py:54
  51.3 25.2 %all-to-all-start.1 = ((bf16[8,32,1024]{2,1,0:T(8,128)(2,1)}), bf16[8,32,1024]{2,1,0:T(8,128)(2,1)S(1)}, u32[]{:S(2)}, u32[]{:S(2)}) async-start(bf16[8,32,1024]{2,1,0:T(8,128)(2,1)} %broadcast_in_dim.5), calls=%async_computation.1 | async-start | bytes 1048576 | tf_op jit(solution)/shard_map/all_to_all | solution.py:216
  58.5 28.9 %collective-permute-start.8 = (bf16[4,80,1024]{2,1,0:T(8,128)(2,1)}, bf16[4,80,1024]{2,1,0:T(8,128)(2,1)}, u32[]{:S(2)}, u32[]{:S(2)}) collective-permute-start(bf16[4,80,1024]{2,1,0:T(8,128)(2,1)} %collective-permute-done.7.refs_2_), channel_id=1, source_target_pairs={{0,4},{1,5},{2,6},{3,7},{4,8},{5,9},{6,10},{7,11},{8,12},{9,13},{1... | collective-permute-start | bytes 1966088 | tf_op jit(solution)/shard_map/ppermute | solution.py:54
  65.6 34.9 %collective-permute-start.11 = (bf16[4,80,1024]{2,1,0:T(8,128)(2,1)}, bf16[4,80,1024]{2,1,0:T(8,128)(2,1)}, u32[]{:S(2)}, u32[]{:S(2)}) collective-permute-start(bf16[4,80,1024]{2,1,0:T(8,128)(2,1)} %collective-permute-done.10.refs_5_), channel_id=1, source_target_pairs={{0,28},{1,29},{2,30},{3,31},{4,0},{5,1},{6,2},{7,3},{8,4},{9,5},{1... | collective-permute-start | bytes 1966088 | tf_op jit(solution)/shard_map/ppermute | solution.py:54
  76.5 33.8 %collective-permute-start.15 = (bf16[8,32,1024]{2,1,0:T(8,128)(2,1)S(1)}, bf16[8,32,1024]{2,1,0:T(8,128)(2,1)}, u32[]{:S(2)}, u32[]{:S(2)}) collective-permute-start(bf16[8,32,1024]{2,1,0:T(8,128)(2,1)S(1)} %all-to-all-done.1.refs_9_), channel_id=1, source_target_pairs={{0,32},{1,33},{2,34},{3,35},{4,36},{5,37},{6,38},{7,39},{8,40},{9,... | collective-permute-start | bytes 1572872 | tf_op jit(solution)/shard_map/ppermute | solution.py:54
  77.0 33.3 %collective-permute-start.16 = (bf16[8,32,1024]{2,1,0:T(8,128)(2,1)S(1)}, bf16[8,32,1024]{2,1,0:T(8,128)(2,1)}, u32[]{:S(2)}, u32[]{:S(2)}) collective-permute-start(bf16[8,32,1024]{2,1,0:T(8,128)(2,1)S(1)} %all-to-all-done.1.refs_9_), channel_id=1, source_target_pairs={{0,34},{1,35},{2,32},{3,33},{4,38},{5,39},{6,36},{7,37},{8,42},{9,... | collective-permute-start | bytes 1572872 | tf_op jit(solution)/shard_map/ppermute | solution.py:54
  87.3 23.0 %collective-permute-start.17 = (bf16[8,32,1024]{2,1,0:T(8,128)(2,1)S(1)}, bf16[8,32,1024]{2,1,0:T(8,128)(2,1)}, u32[]{:S(2)}, u32[]{:S(2)}) collective-permute-start(bf16[8,32,1024]{2,1,0:T(8,128)(2,1)S(1)} %all-to-all-done.1.refs_9_), channel_id=1, source_target_pairs={{0,2},{1,3},{2,0},{3,1},{4,6},{5,7},{6,4},{7,5},{8,10},{9,11},{10,... | collective-permute-start | bytes 1572872 | tf_op jit(solution)/shard_map/ppermute | solution.py:54
  91.1 15.6 %all-to-all-start = ((f32[32,2,128]{2,1,0:T(2,128)}), f32[32,2,128]{2,1,0:T(2,128)S(1)}, u32[]{:S(2)}, u32[]{:S(2)}) async-start(f32[32,2,128]{2,1,0:T(2,128)} %reshape.127), calls=%async_computation | async-start | bytes 65536 | tf_op jit(solution)/shard_map/all_to_all | solution.py:211
  100.5 15.3 %collective-permute-start.12 = (bf16[4,48,1024]{2,1,0:T(8,128)(2,1)}, bf16[4,48,1024]{2,1,0:T(8,128)(2,1)}, u32[]{:S(2)}, u32[]{:S(2)}) collective-permute-start(bf16[4,48,1024]{2,1,0:T(8,128)(2,1)} %slice.192), channel_id=1, source_target_pairs={{0,4},{1,5},{2,6},{3,7},{4,8},{5,9},{6,10},{7,11},{8,12},{9,13},{1... | collective-permute-start | bytes 1179656 | tf_op jit(solution)/shard_map/ppermute | solution.py:54
  107.9 7.9 %collective-permute-start.13 = (bf16[4,32,1024]{2,1,0:T(8,128)(2,1)S(1)}, bf16[4,32,1024]{2,1,0:T(8,128)(2,1)S(1)}, u32[]{:S(2)}, u32[]{:S(2)}) collective-permute-start(bf16[4,32,1024]{2,1,0:T(8,128)(2,1)S(1)} %slice.193), channel_id=1, source_target_pairs={{0,28},{1,29},{2,30},{3,31},{4,0},{5,1},{6,2},{7,3},{8,4},{9,5},{1... | collective-permute-start | bytes 786440 | tf_op jit(solution)/shard_map/ppermute | solution.py:54
  119.0 2.7 %collective-permute-start.19 = (bf16[512,1024]{1,0:T(8,128)(2,1)S(1)}, bf16[512,1024]{1,0:T(8,128)(2,1)S(1)}, u32[]{:S(2)}, u32[]{:S(2)}) collective-permute-start(bf16[512,1024]{1,0:T(8,128)(2,1)S(1)} %get-tuple-element.26.own), channel_id=1, source_target_pairs={{0,1},{1,0},{2,3},{3,2},{4,5},{5,4},{6,7},{7,6},{8,9},{9,8},{10,11... | collective-permute-start | bytes 3145736 | tf_op jit(solution)/shard_map/ppermute | solution.py:54
  119.1 3.3 %collective-permute-start = (f32[8,1024]{1,0:T(8,128)S(1)}, f32[8,1024]{1,0:T(8,128)S(1)}, u32[]{:S(2)}, u32[]{:S(2)}) collective-permute-start(f32[8,1024]{1,0:T(8,128)S(1)} %reshape.129.refs_13_.own), channel_id=1, source_target_pairs={{0,1},{1,0},{2,3},{3,2},{4,5},{5,4},{6,7},{7,6},{8,9},{9,8},{10,11... | collective-permute-start | bytes 98312 | tf_op jit(solution)/shard_map/ppermute | solution.py:54
  125.3 4.3 %collective-permute-start.20 = (bf16[8,3584]{1,0:T(8,128)(2,1)S(1)}, bf16[8,3584]{1,0:T(8,128)(2,1)S(1)}, u32[]{:S(2)}, u32[]{:S(2)}) collective-permute-start(bf16[8,3584]{1,0:T(8,128)(2,1)S(1)} %pad_maximum_fusion.4), channel_id=1, source_target_pairs={{0,64},{1,65},{2,66},{3,67},{4,68},{5,69},{6,70},{7,71},{8,72},{9,... | collective-permute-start | bytes 172040 | tf_op jit(solution)/shard_map/ppermute | solution.py:54
  133.7 5.4 %collective-permute-start.22 = (bf16[8,3072]{1,0:T(8,128)(2,1)S(1)}, bf16[8,3072]{1,0:T(8,128)(2,1)S(1)}, u32[]{:S(2)}, u32[]{:S(2)}) collective-permute-start(bf16[8,3072]{1,0:T(8,128)(2,1)S(1)} %pad_maximum_fusion.6), channel_id=1, source_target_pairs={{0,192},{1,193},{2,194},{3,195},{4,196},{5,197},{6,198},{7,199},{8... | collective-permute-start | bytes 147464 | tf_op jit(solution)/shard_map/ppermute | solution.py:54
  143.1 4.2 %collective-permute-start.24 = (bf16[8,3072]{1,0:T(8,128)(2,1)S(1)}, bf16[8,3072]{1,0:T(8,128)(2,1)S(1)}, u32[]{:S(2)}, u32[]{:S(2)}) collective-permute-start(bf16[8,3072]{1,0:T(8,128)(2,1)S(1)} %pad_maximum_fusion.7), channel_id=1, source_target_pairs={{0,64},{1,65},{2,66},{3,67},{4,68},{5,69},{6,70},{7,71},{8,72},{9,... | collective-permute-start | bytes 147464 | tf_op jit(solution)/shard_map/ppermute | solution.py:54
  148.1 1.3 collective-permute-start.25
  154.1 4.2 %collective-permute-start.27 = (bf16[8,3072]{1,0:T(8,128)(2,1)S(1)}, bf16[8,3072]{1,0:T(8,128)(2,1)S(1)}, u32[]{:S(2)}, u32[]{:S(2)}) collective-permute-start(bf16[8,3072]{1,0:T(8,128)(2,1)S(1)} %pad_maximum_fusion.8), channel_id=1, source_target_pairs={{0,64},{1,65},{2,66},{3,67},{4,68},{5,69},{6,70},{7,71},{8,72},{9,... | collective-permute-start | bytes 147464 | tf_op jit(solution)/shard_map/ppermute | solution.py:54
  159.8 1.3 collective-permute-start.28
  162.1 5.4 %collective-permute-start.29 = (bf16[8,3072]{1,0:T(8,128)(2,1)S(1)}, bf16[8,3072]{1,0:T(8,128)(2,1)S(1)}, u32[]{:S(2)}, u32[]{:S(2)}) collective-permute-start(bf16[8,3072]{1,0:T(8,128)(2,1)S(1)} %pad_maximum_fusion.9), channel_id=1, source_target_pairs={{0,192},{1,193},{2,194},{3,195},{4,196},{5,197},{6,198},{7,199},{8... | collective-permute-start | bytes 147464 | tf_op jit(solution)/shard_map/ppermute | solution.py:54
  169.1 1.3 collective-permute-start.30
  171.3 4.3 %collective-permute-start.31 = (bf16[8,3584]{1,0:T(8,128)(2,1)S(1)}, bf16[8,3584]{1,0:T(8,128)(2,1)S(1)}, u32[]{:S(2)}, u32[]{:S(2)}) collective-permute-start(bf16[8,3584]{1,0:T(8,128)(2,1)S(1)} %pad_maximum_fusion.5), channel_id=1, source_target_pairs={{0,64},{1,65},{2,66},{3,67},{4,68},{5,69},{6,70},{7,71},{8,72},{9,... | collective-permute-start | bytes 172040 | tf_op jit(solution)/shard_map/ppermute | solution.py:54
  177.2 1.3 collective-permute-start.32
  (6 other events, 9.7 us)
where the time goes:
time: 204 us; the launch traced here: 200 us
  waiting for transfers between devices  85.6 us (42%)
  starting transfers between devices  53.9 us (26%)
  Pallas kernels  22.2 us (11%)
  blocking collectives  18.4 us (9%)
  local copies, waits for them, and re-layouts  9.07 us (4%)
  matrix products  7.87 us (4%)
  other arithmetic  2.26 us (1%)
    ppermute x33, waiting for transfers between devices, send(): return lax.ppermute(x, BOTH, pairs)  74 us
    ppermute x33, starting transfers between devices, send(): return lax.ppermute(x, BOTH, pairs)  38.2 us
    pallas_call x13, Pallas kernels, call(): pl.pallas_call(body, out_shape=out, in_specs=specs, out_specs=[pl.BlockSp...  22.2 us
    all_to_all x1, blocking collectives, solve(): got = lax.all_to_all(final, 'row', 0, 0, tiled=True).astype(F32)  18.4 us
    dot_general x6, matrix products, dot(): return lax.dot_general(a, b, dims, preferred_element_type=F32)  7.87 us
    all_to_all x1, starting transfers between devices, solve(): lax.all_to_all(lanes, BOTH, 0, 0, axis_index_groups=PLANES, tiled=True)  7.66 us
    all_to_all x1, waiting for transfers between devices, solve(): lax.all_to_all(jnp.broadcast_to(skip, (8, rows, width)), BOTH, 0, 0, axis...  6.96 us
    all_to_all x1, starting transfers between devices, solve(): lax.all_to_all(jnp.broadcast_to(skip, (8, rows, width)), BOTH, 0, 0, axis...  5.85 us
  transfers between devices with their start and end apart: 36, of which 26 were waited for; matrix products, arithmetic and copies ran while one was open for 4% of the time, Pallas kernels for 0%

commit v1 on v0

--- a/solution.py
+++ b/solution.py
@@ -123,7 +123,7 @@
     return jnp.concatenate([low, high], axis=1)
 
 
-def forward_body(stage, ids, own, other, old, near, jump, tied, near_from, jump_from, *outs):
+def forward_body(stage, ids, own, other, old, near, jump, tied, near_from, *outs):
     y, core = ids[0], ids[4]
     half = own.shape[1] // 2
     width = 2 * half
@@ -135,22 +135,35 @@
     if stage == 3:
         return
     source = kept if stage < 2 else jnp.where(y == 3, near_from[...], kept)
-    for t in range(2):
+
+    def section(t, carry):
         total = dot(source[:, :width], near[t, 0], NT) + dot(source[:, width:], near[t, 1], NT)
-        outs[1][:, t * half : (t + 1) * half] = total
-    source = kept if stage == 0 else jump_from[...]
-    outs[1][:, width:] = dot(source[:, :width], jump[0], NT) + dot(source[:, width:], jump[1], NT)
-
-
-def products_body(ids, near_from, jump_from, near, jump, by_near, by_jump):
-    half = near_from.shape[1] // 2
+        outs[1][:, pl.ds(pl.multiple_of(t * half, half), half)] = total
+        return carry
+
+    lax.fori_loop(0, 2, section, 0)
+    if stage == 0:
+        outs[1][:, width:] = dot(kept[:, :width], jump[0], NT) + dot(kept[:, width:], jump[1], NT)
+
+
+def near_body(ids, source, near, out):
+    half = source.shape[1] // 2
     width = 2 * half
-    a, b = near_from[:, :half], near_from[:, half:]
+    a, b = source[:, :half], source[:, half:]
 
     def column(c, carry):
         at = pl.ds(pl.multiple_of(c * width, width), width)
-        by_near[:, at] = dot(a, near[0, c], NN) + dot(b, near[1, c], NN)
-        by_jump[:, at] = dot(jump_from[...], jump[c], NN)
+        out[:, at] = dot(a, near[0, c], NN) + dot(b, near[1, c], NN)
+        return carry
+
+    lax.fori_loop(0, 2, column, 0)
+
+
+def jump_body(ids, source, jump, out):
+    width = jump.shape[2]
+
+    def column(c, carry):
+        out[:, pl.ds(pl.multiple_of(c * width, width), width)] = dot(source[...], jump[c], NN)
         return carry
 
     lax.fori_loop(0, 2, column, 0)
@@ -192,17 +205,17 @@
     i, rest = slot % rows, slot // rows
     natural = ((rest % 8) * 4 + ((rest // 8) % 2) * 2 + rest // 16) * rows + i
     pick = (jnp.arange(width)[:, None] == natural[None, :]).astype(BF)
+    m = dot(coupling.reshape(SEC * rows, width), diag_inverse[0], NN).astype(BF)
+    m = dot(m, pick, NN).astype(BF).reshape(SEC, rows, width)
     inverse = dot(diag_inverse[0], pick, NN).astype(BF)
-    m = dot(coupling.reshape(SEC * rows, width), inverse, NN).astype(BF)
-    m = m.reshape(SEC, rows, width)
 
     def blocks(first, count):
         return lax.dynamic_slice_in_dim(m, first, count, 0)
 
     far = send(m[6:8], YB)
-    close = lax.ppermute(blocks(5 + 2 * (y % 2), 1), "sec", [(0, 2), (1, 3), (2, 6), (3, 7)])
     inner = blocks(2 * y + 1, 1)[0]
     given = send(inner[rows // 2 :], XL)
+    close = lax.ppermute(blocks(5 + 2 * (y % 2), 1), "sec", [(0, 2), (1, 3), (2, 6), (3, 7)])
     next_pair = jnp.where(y == 3, far, blocks(jnp.minimum(2 * y + 2, 6), 2))
     skip = jnp.where(y == 0, m[4], jnp.where(y == 2, far[0], close[0]))
     inner = jnp.where(xl == 0, inner[: rows // 2], given)
@@ -230,14 +243,18 @@
     zero_z = jnp.zeros((cols, 2 * width), BF)
     kept, got_z, resid, stash, ours = zero_z, zero_z, mine, None, None
     for stage in range(4):
-        shapes = [struct(2 * width, BF)] + ([struct(width + half, F32)] if stage < 3 else [])
-        got = call(
-            functools.partial(forward_body, stage), shapes, ids, resid, send(resid, CORE), kept, near, jump, tied, got_z, got_z
-        )
+        shapes = [struct(2 * width, BF)]
+        shapes += [struct(width + half if stage == 0 else width, F32)] if stage < 3 else []
+        across = send(resid, CORE)
+        if 0 < stage < 3:
+            leap = dot(got_z[:, :width], jump[0], NT) + dot(got_z[:, width:], jump[1], NT)
+        got = call(functools.partial(forward_body, stage), shapes, ids, resid, across, kept, near, jump, tied, got_z)
         kept = got[0]
         if stage == 3:
             break
-        update, leap = got[1][:, :width], got[1][:, width:]
+        update = got[1][:, :width]
+        if stage == 0:
+            leap = got[1][:, width:]
         if stage == 0:
             sent = jnp.concatenate([update.astype(BF), leap.astype(BF), kept], axis=1)
         elif stage == 1:
@@ -277,7 +294,8 @@
                 sources = got_x, got_x[:, half:]
             else:
                 sources = got_x, arrived[:, 3 * width :]
-            by_near, by_jump = call(products_body, [struct(2 * width, F32)] * 2, ids, *sources, near, jump)
+            by_near = call(near_body, struct(2 * width, F32), ids, sources[0], near)
+            by_jump = call(jump_body, struct(2 * width, F32), ids, sources[1], jump)
             if stage == 1:
                 own = by_near
                 give = jnp.where(y == 3, by_near, by_jump + got_c)

time: 204 us -> 204 us (level)
  waiting for transfers between devices: 85.6 us -> 81 us
    ppermute x33, waiting for transfers between devices: 74 us -> 69.5 us  [send(): return lax.ppermute(x, BOTH, pairs)]
    pallas_call x13 -> x16, Pallas kernels: 22.2 us -> 24.2 us  [call(): pl.pallas_call(body, out_shape=out, in_specs=specs, out_specs=[pl.BlockSp...]
    dot_general x6 -> x10, matrix products: 7.87 us -> 9.55 us  [dot(): return lax.dot_general(a, b, dims, preferred_element_type=F32)]
  transfers between devices with their start and end apart: 36 -> 36, of which waited for: 26 -> 25; matrix products, arithmetic and copies ran while one was open for 4% -> 6% of each run, Pallas kernels for 0% -> 1%
where the time goes in v1:
time: 204 us; the launch traced here: 201 us
  waiting for transfers between devices  81 us (40%)
  starting transfers between devices  54.9 us (27%)
  Pallas kernels  24.2 us (12%)
  blocking collectives  18.3 us (9%)
  matrix products  9.55 us (5%)
  local copies, waits for them, and re-layouts  9.08 us (4%)
  other arithmetic  2.26 us (1%)
    ppermute x33, waiting for transfers between devices, send(): return lax.ppermute(x, BOTH, pairs)  69.5 us
    ppermute x33, starting transfers between devices, send(): return lax.ppermute(x, BOTH, pairs)  39.2 us
    pallas_call x16, Pallas kernels, call(): pl.pallas_call(body, out_shape=out, in_specs=specs, out_specs=[pl.BlockSp...  24.2 us
    all_to_all x1, blocking collectives, solve(): got = lax.all_to_all(final, 'row', 0, 0, tiled=True).astype(F32)  18.3 us
    dot_general x10, matrix products, dot(): return lax.dot_general(a, b, dims, preferred_element_type=F32)  9.55 us
    all_to_all x1, starting transfers between devices, solve(): lax.all_to_all(lanes, BOTH, 0, 0, axis_index_groups=PLANES, tiled=True)  7.66 us
    all_to_all x1, waiting for transfers between devices, solve(): lax.all_to_all(jnp.broadcast_to(skip, (8, rows, width)), BOTH, 0, 0, axis...  6.97 us
    all_to_all x1, starting transfers between devices, solve(): lax.all_to_all(jnp.broadcast_to(skip, (8, rows, width)), BOTH, 0, 0, axis...  5.83 us
  transfers between devices with their start and end apart: 36, of which 25 were waited for; matrix products, arithmetic and copies ran while one was open for 6% of the time, Pallas kernels for 1%

profile of v1, /device:TPU:4, one launch (start us, length us, event | category | flops | bytes accessed | tf_op | source)
XLA Modules:
  0.0 200.5 jit_solution(12545780641960515783)
XLA Ops:
  2.2 2.5 %fusion.12 = bf16[256,1024]{1,0:T(8,128)(2,1)S(1)} fusion(s32[1024]{0:T(1024)S(1)} %fusion.55, bf16[256,1024]{1,0:T(8,128)(2,1)} %bitcast.90, bf16[1,1024,1024]{2,1,0:T(8,128)(2,1)S(1)} %copy-done), kind=kOutput, calls=%fused_computation.11 | convolution fusion | flops 1075314688 | bytes 3149824 | tf_op jit(solution)/shard_map/dot_general | solution.py:58
  6.0 3.1 %collective-permute-start.1 = (bf16[2,32,1024]{2,1,0:T(8,128)(2,1)S(1)}, bf16[2,32,1024]{2,1,0:T(8,128)(2,1)S(1)}, u32[]{:S(2)}, u32[]{:S(2)}) collective-permute-start(bf16[2,32,1024]{2,1,0:T(8,128)(2,1)S(1)} %bitcast.89), channel_id=1, source_target_pairs={{0,192},{1,193},{2,194},{3,195},{4,196},{5,197},{6,198},{7,199},{8... | collective-permute-start | bytes 393224 | tf_op jit(solution)/shard_map/ppermute | solution.py:54
  9.1 3.2 %collective-permute-done.1 = bf16[2,32,1024]{2,1,0:T(8,128)(2,1)S(1)} collective-permute-done((bf16[2,32,1024]{2,1,0:T(8,128)(2,1)S(1)}, bf16[2,32,1024]{2,1,0:T(8,128)(2,1)S(1)}, u32[]{:S(2)}, u32[]{:S(2)}) %collective-permute-start.1) | collective-permute-done | bytes 131104 | tf_op jit(solution)/shard_map/ppermute | solution.py:54
  16.7 2.3 %collective-permute-done.3 = bf16[80,1024]{1,0:T(8,128)(2,1)S(1)} collective-permute-done((bf16[80,1024]{1,0:T(8,128)(2,1)S(1)}, bf16[80,1024]{1,0:T(8,128)(2,1)S(1)}, u32[]{:S(2)}, u32[]{:S(2)}) %collective-permute-start.3) | collective-permute-done | bytes 163872 | tf_op jit(solution)/shard_map/ppermute | solution.py:54
  19.6 2.4 %collective-permute-done.5 = bf16[80,1024]{1,0:T(8,128)(2,1)S(1)} collective-permute-done((bf16[80,1024]{1,0:T(8,128)(2,1)S(1)}, bf16[80,1024]{1,0:T(8,128)(2,1)S(1)}, u32[]{:S(2)}, u32[]{:S(2)}) %collective-permute-start.5) | collective-permute-done | bytes 163872 | tf_op jit(solution)/shard_map/ppermute | solution.py:54
  23.4 3.8 %convert_bitcast_fusion = bf16[1024,1024]{1,0:T(8,128)(2,1)} fusion(bf16[1,1024,1024]{2,1,0:T(8,128)(2,1)S(1)} %copy-done, s32[1024]{0:T(1024)S(1)} %fusion.55), kind=kOutput, calls=%fused_computation.6 | convolution fusion | flops 2149580800 | bytes 4198400 | tf_op jit(solution)/shard_map/dot_general | solution.py:58
  29.1 4.0 %collective-permute-start.9 = (bf16[4,80,1024]{2,1,0:T(8,128)(2,1)S(1)}, bf16[4,80,1024]{2,1,0:T(8,128)(2,1)}, u32[]{:S(2)}, u32[]{:S(2)}) collective-permute-start(bf16[4,80,1024]{2,1,0:T(8,128)(2,1)S(1)} %pad_maximum_fusion.refs_0_), channel_id=1, source_target_pairs={{0,28},{1,29},{2,30},{3,31},{4,0},{5,1},{6,2},{7,3},{8,4},{9,5},{1... | collective-permute-start | bytes 1966088 | tf_op jit(solution)/shard_map/ppermute | solution.py:54
  33.1 6.7 %collective-permute-done.6.refs_1_ = bf16[4,80,1024]{2,1,0:T(8,128)(2,1)} collective-permute-done((bf16[4,80,1024]{2,1,0:T(8,128)(2,1)S(1)}, bf16[4,80,1024]{2,1,0:T(8,128)(2,1)}, u32[]{:S(2)}, u32[]{:S(2)}) %collective-permute-start.6) | collective-permute-done | bytes 655392 | tf_op jit(solution)/shard_map/ppermute | solution.py:54
  42.0 4.6 %collective-permute-done.9.refs_4_ = bf16[4,80,1024]{2,1,0:T(8,128)(2,1)} collective-permute-done((bf16[4,80,1024]{2,1,0:T(8,128)(2,1)S(1)}, bf16[4,80,1024]{2,1,0:T(8,128)(2,1)}, u32[]{:S(2)}, u32[]{:S(2)}) %collective-permute-start.9) | collective-permute-done | bytes 655392 | tf_op jit(solution)/shard_map/ppermute | solution.py:54
  46.7 3.8 %collective-permute-start.10 = (bf16[4,80,1024]{2,1,0:T(8,128)(2,1)}, bf16[4,80,1024]{2,1,0:T(8,128)(2,1)}, u32[]{:S(2)}, u32[]{:S(2)}) collective-permute-start(bf16[4,80,1024]{2,1,0:T(8,128)(2,1)} %collective-permute-done.9.refs_4_), channel_id=1, source_target_pairs={{0,28},{1,29},{2,30},{3,31},{4,0},{5,1},{6,2},{7,3},{8,4},{9,5},{1... | collective-permute-start | bytes 1966088 | tf_op jit(solution)/shard_map/ppermute | solution.py:54
  51.4 5.8 %all-to-all-start.1 = ((bf16[8,32,1024]{2,1,0:T(8,128)(2,1)}), bf16[8,32,1024]{2,1,0:T(8,128)(2,1)S(1)}, u32[]{:S(2)}, u32[]{:S(2)}) async-start(bf16[8,32,1024]{2,1,0:T(8,128)(2,1)} %broadcast_in_dim.5), calls=%async_computation.1 | async-start | bytes 1048576 | tf_op jit(solution)/shard_map/all_to_all | solution.py:229
  59.2 6.4 %collective-permute-done.10.refs_5_ = bf16[4,80,1024]{2,1,0:T(8,128)(2,1)} collective-permute-done((bf16[4,80,1024]{2,1,0:T(8,128)(2,1)}, bf16[4,80,1024]{2,1,0:T(8,128)(2,1)}, u32[]{:S(2)}, u32[]{:S(2)}) %collective-permute-start.10) | collective-permute-done | bytes 655392 | tf_op jit(solution)/shard_map/ppermute | solution.py:54
  65.7 3.9 %collective-permute-start.11 = (bf16[4,80,1024]{2,1,0:T(8,128)(2,1)}, bf16[4,80,1024]{2,1,0:T(8,128)(2,1)}, u32[]{:S(2)}, u32[]{:S(2)}) collective-permute-start(bf16[4,80,1024]{2,1,0:T(8,128)(2,1)} %collective-permute-done.10.refs_5_), channel_id=1, source_target_pairs={{0,28},{1,29},{2,30},{3,31},{4,0},{5,1},{6,2},{7,3},{8,4},{9,5},{1... | collective-permute-start | bytes 1966088 | tf_op jit(solution)/shard_map/ppermute | solution.py:54
  69.6 7.0 %all-to-all-done.1.refs_9_ = bf16[8,32,1024]{2,1,0:T(8,128)(2,1)S(1)} async-done(((bf16[8,32,1024]{2,1,0:T(8,128)(2,1)}), bf16[8,32,1024]{2,1,0:T(8,128)(2,1)S(1)}, u32[]{:S(2)}, u32[]{:S(2)}) %all-to-all-start.1) | async-done | bytes 524320 | tf_op jit(solution)/shard_map/all_to_all | solution.py:229
  78.6 8.8 %collective-permute-done.8.refs_3_ = bf16[4,80,1024]{2,1,0:T(8,128)(2,1)} collective-permute-done((bf16[4,80,1024]{2,1,0:T(8,128)(2,1)}, bf16[4,80,1024]{2,1,0:T(8,128)(2,1)}, u32[]{:S(2)}, u32[]{:S(2)}) %collective-permute-start.8) | collective-permute-done | bytes 655392 | tf_op jit(solution)/shard_map/ppermute | solution.py:54
  87.4 2.2 %collective-permute-start.17 = (bf16[8,32,1024]{2,1,0:T(8,128)(2,1)S(1)}, bf16[8,32,1024]{2,1,0:T(8,128)(2,1)}, u32[]{:S(2)}, u32[]{:S(2)}) collective-permute-start(bf16[8,32,1024]{2,1,0:T(8,128)(2,1)S(1)} %all-to-all-done.1.refs_9_), channel_id=1, source_target_pairs={{0,2},{1,3},{2,0},{3,1},{4,6},{5,7},{6,4},{7,5},{8,10},{9,11},{10,... | collective-permute-start | bytes 1572872 | tf_op jit(solution)/shard_map/ppermute | solution.py:54
  91.3 7.7 %all-to-all-start = ((f32[32,2,128]{2,1,0:T(2,128)}), f32[32,2,128]{2,1,0:T(2,128)S(1)}, u32[]{:S(2)}, u32[]{:S(2)}) async-start(f32[32,2,128]{2,1,0:T(2,128)} %reshape.127), calls=%async_computation | async-start | bytes 65536 | tf_op jit(solution)/shard_map/all_to_all | solution.py:224
  102.3 4.5 %all-to-all-done = f32[32,2,128]{2,1,0:T(2,128)S(1)} async-done(((f32[32,2,128]{2,1,0:T(2,128)}), f32[32,2,128]{2,1,0:T(2,128)S(1)}, u32[]{:S(2)}, u32[]{:S(2)}) %all-to-all-start) | async-done | bytes 32800 | tf_op jit(solution)/shard_map/all_to_all | solution.py:224
  110.5 5.5 %collective-permute-done.13.refs_8_ = bf16[4,32,1024]{2,1,0:T(8,128)(2,1)S(1)} collective-permute-done((bf16[4,32,1024]{2,1,0:T(8,128)(2,1)S(1)}, bf16[4,32,1024]{2,1,0:T(8,128)(2,1)S(1)}, u32[]{:S(2)}, u32[]{:S(2)}) %collective-permute-start.13) | collective-permute-done | bytes 262176 | tf_op jit(solution)/shard_map/ppermute | solution.py:54
  116.0 3.2 %shard_map.50 = (bf16[2,2,512,1024]{3,2,1,0:T(8,128)(2,1)S(1)}, bf16[2,512,1024]{2,1,0:T(8,128)(2,1)S(1)}, bf16[512,1024]{1,0:T(8,128)(2,1)S(1)}) custom-call(s32[5]{0:T(128)S(1)} %stack.38.ids, bf16[4,80,1024]{2,1,0:T(8,128)(2,1)S(1)} %pad_maximum_fusion.refs_0_, bf16[4,80,1024]{2,1,0:T(8,128)(2,1)} %collective-permute-done.6.refs_1_, ...), custom_call_target="tpu_custom_call" | custom-call | tf_op jit(solution)/shard_map/pallas_call | solution.py:65
  122.7 3.1 %shard_map.52 = (bf16[8,2048]{1,0:T(8,128)(2,1)S(1)}, f32[8,1536]{1,0:T(8,128)S(1)}) custom-call(s32[5]{0:T(128)S(1)} %stack.38.ids, f32[8,1024]{1,0:T(8,128)S(1)} %reshape.129.refs_13_.own, f32[8,1024]{1,0:T(8,128)S(1)} %collective-permute-done.other, bf16[8,2048]{1,0:T(8,128)(2,1)S(1)} %broadcast_5_old_near_from_own_other.2.old.near_from.own.other, ...), custom_call_target="tpu_custom_call" | custom-call | tf_op jit(solution)/shard_map/pallas_call | solution.py:65
  126.0 4.2 %collective-permute-done.20 = bf16[8,3584]{1,0:T(8,128)(2,1)S(1)} collective-permute-done((bf16[8,3584]{1,0:T(8,128)(2,1)S(1)}, bf16[8,3584]{1,0:T(8,128)(2,1)S(1)}, u32[]{:S(2)}, u32[]{:S(2)}) %collective-permute-start.20) | collective-permute-done | bytes 57376 | tf_op jit(solution)/shard_map/ppermute | solution.py:54
  131.4 2.5 %shard_map.53 = (bf16[8,2048]{1,0:T(8,128)(2,1)S(1)}, f32[8,1024]{1,0:T(8,128)S(1)}) custom-call(s32[5]{0:T(128)S(1)} %stack.38.ids, f32[8,1024]{1,0:T(8,128)S(1)} %convert_subtract_fusion.1.own, f32[8,1024]{1,0:T(8,128)S(1)} %collective-permute-done.21.other, bf16[8,2048]{1,0:T(8,128)(2,1)S(1)} %get-tuple-element.22.old, ...), custom_call_target="tpu_custom_call" | custom-call | tf_op jit(solution)/shard_map/pallas_call | solution.py:65
  133.9 2.6 %collective-permute-start.22 = (bf16[8,3072]{1,0:T(8,128)(2,1)S(1)}, bf16[8,3072]{1,0:T(8,128)(2,1)S(1)}, u32[]{:S(2)}, u32[]{:S(2)}) collective-permute-start(bf16[8,3072]{1,0:T(8,128)(2,1)S(1)} %pad_maximum_fusion.6), channel_id=1, source_target_pairs={{0,192},{1,193},{2,194},{3,195},{4,196},{5,197},{6,198},{7,199},{8... | collective-permute-start | bytes 147464 | tf_op jit(solution)/shard_map/ppermute | solution.py:54
  136.5 2.8 %collective-permute-done.22 = bf16[8,3072]{1,0:T(8,128)(2,1)S(1)} collective-permute-done((bf16[8,3072]{1,0:T(8,128)(2,1)S(1)}, bf16[8,3072]{1,0:T(8,128)(2,1)S(1)}, u32[]{:S(2)}, u32[]{:S(2)}) %collective-permute-start.22) | collective-permute-done | bytes 49184 | tf_op jit(solution)/shard_map/ppermute | solution.py:54
  140.5 2.5 %shard_map.54 = (bf16[8,2048]{1,0:T(8,128)(2,1)S(1)}, f32[8,1024]{1,0:T(8,128)S(1)}) custom-call(s32[5]{0:T(128)S(1)} %stack.38.ids, f32[8,1024]{1,0:T(8,128)S(1)} %convert_subtract_fusion.own, f32[8,1024]{1,0:T(8,128)S(1)} %collective-permute-done.23.other, bf16[8,2048]{1,0:T(8,128)(2,1)S(1)} %get-tuple-element.24.old, ...), custom_call_target="tpu_custom_call" | custom-call | tf_op jit(solution)/shard_map/pallas_call | solution.py:65
  143.1 4.1 %collective-permute-done.24 = bf16[8,3072]{1,0:T(8,128)(2,1)S(1)} collective-permute-done((bf16[8,3072]{1,0:T(8,128)(2,1)S(1)}, bf16[8,3072]{1,0:T(8,128)(2,1)S(1)}, u32[]{:S(2)}, u32[]{:S(2)}) %collective-permute-start.24) | collective-permute-done | bytes 49184 | tf_op jit(solution)/shard_map/ppermute | solution.py:54
  154.1 4.1 %collective-permute-done.27 = bf16[8,3072]{1,0:T(8,128)(2,1)S(1)} collective-permute-done((bf16[8,3072]{1,0:T(8,128)(2,1)S(1)}, bf16[8,3072]{1,0:T(8,128)(2,1)S(1)}, u32[]{:S(2)}, u32[]{:S(2)}) %collective-permute-start.27) | collective-permute-done | bytes 49184 | tf_op jit(solution)/shard_map/ppermute | solution.py:54
  161.7 2.6 %collective-permute-start.29 = (bf16[8,3072]{1,0:T(8,128)(2,1)S(1)}, bf16[8,3072]{1,0:T(8,128)(2,1)S(1)}, u32[]{:S(2)}, u32[]{:S(2)}) collective-permute-start(bf16[8,3072]{1,0:T(8,128)(2,1)S(1)} %pad_maximum_fusion.9), channel_id=1, source_target_pairs={{0,192},{1,193},{2,194},{3,195},{4,196},{5,197},{6,198},{7,199},{8... | collective-permute-start | bytes 147464 | tf_op jit(solution)/shard_map/ppermute | solution.py:54
  164.3 2.8 %collective-permute-done.29 = bf16[8,3072]{1,0:T(8,128)(2,1)S(1)} collective-permute-done((bf16[8,3072]{1,0:T(8,128)(2,1)S(1)}, bf16[8,3072]{1,0:T(8,128)(2,1)S(1)}, u32[]{:S(2)}, u32[]{:S(2)}) %collective-permute-start.29) | collective-permute-done | bytes 49184 | tf_op jit(solution)/shard_map/ppermute | solution.py:54
  170.8 4.2 %collective-permute-done.31 = bf16[8,3584]{1,0:T(8,128)(2,1)S(1)} collective-permute-done((bf16[8,3584]{1,0:T(8,128)(2,1)S(1)}, bf16[8,3584]{1,0:T(8,128)(2,1)S(1)}, u32[]{:S(2)}, u32[]{:S(2)}) %collective-permute-start.31) | collective-permute-done | bytes 57376 | tf_op jit(solution)/shard_map/ppermute | solution.py:54
  180.7 18.3 %all_to_all.15 = bf16[32,4,128]{2,1,0:T(4,128)(2,1)S(1)} all-to-all(bf16[32,4,128]{2,1,0:T(4,128)(2,1)S(1)} %reshape.136), channel_id=1, replica_groups=mesh['sec'=8,'row'=32] {'row'}, dimensions={0} | all-to-all | bytes 65536 | tf_op jit(solution)/shard_map/all_to_all | solution.py:325
  (135 shorter events, 54.1 us)
Async XLA Ops:
  4.7 4.4 %collective-permute-start.2 = (bf16[16,1024]{1,0:T(8,128)(2,1)S(1)}, bf16[16,1024]{1,0:T(8,128)(2,1)S(1)}, u32[]{:S(2)}, u32[]{:S(2)}) collective-permute-start(bf16[16,1024]{1,0:T(8,128)(2,1)S(1)} %dynamic-slice_bitcast_fusion), channel_id=1, source_target_pairs={{0,32},{1,33},{2,34},{3,35},{4,36},{5,37},{6,38},{7,39},{8,40},{9,... | collective-permute-start | bytes 98312 | tf_op jit(solution)/shard_map/ppermute | solution.py:54
  6.0 6.3 %collective-permute-start.1 = (bf16[2,32,1024]{2,1,0:T(8,128)(2,1)S(1)}, bf16[2,32,1024]{2,1,0:T(8,128)(2,1)S(1)}, u32[]{:S(2)}, u32[]{:S(2)}) collective-permute-start(bf16[2,32,1024]{2,1,0:T(8,128)(2,1)S(1)} %bitcast.89), channel_id=1, source_target_pairs={{0,192},{1,193},{2,194},{3,195},{4,196},{5,197},{6,198},{7,199},{8... | collective-permute-start | bytes 393224 | tf_op jit(solution)/shard_map/ppermute | solution.py:54
  12.4 6.6 %collective-permute-start.3 = (bf16[80,1024]{1,0:T(8,128)(2,1)S(1)}, bf16[80,1024]{1,0:T(8,128)(2,1)S(1)}, u32[]{:S(2)}, u32[]{:S(2)}) collective-permute-start(bf16[80,1024]{1,0:T(8,128)(2,1)S(1)} %get-tuple-element.39), channel_id=1, source_target_pairs={{0,32},{1,33},{2,34},{3,35},{4,36},{5,37},{6,38},{7,39},{8,40},{9,... | collective-permute-start | bytes 491528 | tf_op jit(solution)/shard_map/ppermute | solution.py:54
  13.3 6.3 %collective-permute-start.4 = (bf16[80,1024]{1,0:T(8,128)(2,1)S(1)}, bf16[80,1024]{1,0:T(8,128)(2,1)S(1)}, u32[]{:S(2)}, u32[]{:S(2)}) collective-permute-start(bf16[80,1024]{1,0:T(8,128)(2,1)S(1)} %get-tuple-element.39), channel_id=1, source_target_pairs={{0,34},{1,35},{2,32},{3,33},{4,38},{5,39},{6,36},{7,37},{8,42},{9,... | collective-permute-start | bytes 491528 | tf_op jit(solution)/shard_map/ppermute | solution.py:54
  14.5 7.6 %collective-permute-start.5 = (bf16[80,1024]{1,0:T(8,128)(2,1)S(1)}, bf16[80,1024]{1,0:T(8,128)(2,1)S(1)}, u32[]{:S(2)}, u32[]{:S(2)}) collective-permute-start(bf16[80,1024]{1,0:T(8,128)(2,1)S(1)} %get-tuple-element.39), channel_id=1, source_target_pairs={{0,2},{1,3},{2,0},{3,1},{4,6},{5,7},{6,4},{7,5},{8,10},{9,11},{10,... | collective-permute-start | bytes 491528 | tf_op jit(solution)/shard_map/ppermute | solution.py:54
  22.1 17.6 %collective-permute-start.6 = (bf16[4,80,1024]{2,1,0:T(8,128)(2,1)S(1)}, bf16[4,80,1024]{2,1,0:T(8,128)(2,1)}, u32[]{:S(2)}, u32[]{:S(2)}) collective-permute-start(bf16[4,80,1024]{2,1,0:T(8,128)(2,1)S(1)} %pad_maximum_fusion.refs_0_), channel_id=1, source_target_pairs={{0,4},{1,5},{2,6},{3,7},{4,8},{5,9},{6,10},{7,11},{8,12},{9,13},{1... | collective-permute-start | bytes 1966088 | tf_op jit(solution)/shard_map/ppermute | solution.py:54
  27.2 80.9 %collective-permute-start.18 = (bf16[1024,1024]{1,0:T(8,128)(2,1)}, bf16[1024,1024]{1,0:T(8,128)(2,1)}, u32[]{:S(2)}, u32[]{:S(2)}) collective-permute-start(bf16[1024,1024]{1,0:T(8,128)(2,1)} %convert_bitcast_fusion), channel_id=1, source_target_pairs={{1,32},{3,34},{5,36},{7,38},{9,40},{11,42},{13,44},{15,46},{17,48}... | collective-permute-start | bytes 6291464 | tf_op jit(solution)/shard_map/ppermute | solution.py:54
  29.1 17.5 %collective-permute-start.9 = (bf16[4,80,1024]{2,1,0:T(8,128)(2,1)S(1)}, bf16[4,80,1024]{2,1,0:T(8,128)(2,1)}, u32[]{:S(2)}, u32[]{:S(2)}) collective-permute-start(bf16[4,80,1024]{2,1,0:T(8,128)(2,1)S(1)} %pad_maximum_fusion.refs_0_), channel_id=1, source_target_pairs={{0,28},{1,29},{2,30},{3,31},{4,0},{5,1},{6,2},{7,3},{8,4},{9,5},{1... | collective-permute-start | bytes 1966088 | tf_op jit(solution)/shard_map/ppermute | solution.py:54
  39.8 17.4 %collective-permute-start.7 = (bf16[4,80,1024]{2,1,0:T(8,128)(2,1)}, bf16[4,80,1024]{2,1,0:T(8,128)(2,1)}, u32[]{:S(2)}, u32[]{:S(2)}) collective-permute-start(bf16[4,80,1024]{2,1,0:T(8,128)(2,1)} %collective-permute-done.6.refs_1_), channel_id=1, source_target_pairs={{0,4},{1,5},{2,6},{3,7},{4,8},{5,9},{6,10},{7,11},{8,12},{9,13},{1... | collective-permute-start | bytes 1966088 | tf_op jit(solution)/shard_map/ppermute | solution.py:54
  39.8 10.7 %collective-permute-start.14 = (bf16[1,32,1024]{2,1,0:T(8,128)(2,1)S(1)}, bf16[1,32,1024]{2,1,0:T(8,128)(2,1)S(1)}, u32[]{:S(2)}, u32[]{:S(2)}) collective-permute-start(bf16[1,32,1024]{2,1,0:T(8,128)(2,1)S(1)} %constant_dynamic-slice_fusion), channel_id=1, source_target_pairs={{0,64},{32,96},{64,192},{96,224},{1,65},{33,97},{65,193},{97,225},... | collective-permute-start | bytes 196616 | tf_op jit(solution)/shard_map/ppermute | solution.py:218
  46.7 19.0 %collective-permute-start.10 = (bf16[4,80,1024]{2,1,0:T(8,128)(2,1)}, bf16[4,80,1024]{2,1,0:T(8,128)(2,1)}, u32[]{:S(2)}, u32[]{:S(2)}) collective-permute-start(bf16[4,80,1024]{2,1,0:T(8,128)(2,1)} %collective-permute-done.9.refs_4_), channel_id=1, source_target_pairs={{0,28},{1,29},{2,30},{3,31},{4,0},{5,1},{6,2},{7,3},{8,4},{9,5},{1... | collective-permute-start | bytes 1966088 | tf_op jit(solution)/shard_map/ppermute | solution.py:54
  51.4 25.2 %all-to-all-start.1 = ((bf16[8,32,1024]{2,1,0:T(8,128)(2,1)}), bf16[8,32,1024]{2,1,0:T(8,128)(2,1)S(1)}, u32[]{:S(2)}, u32[]{:S(2)}) async-start(bf16[8,32,1024]{2,1,0:T(8,128)(2,1)} %broadcast_in_dim.5), calls=%async_computation.1 | async-start | bytes 1048576 | tf_op jit(solution)/shard_map/all_to_all | solution.py:229
  57.2 30.2 %collective-permute-start.8 = (bf16[4,80,1024]{2,1,0:T(8,128)(2,1)}, bf16[4,80,1024]{2,1,0:T(8,128)(2,1)}, u32[]{:S(2)}, u32[]{:S(2)}) collective-permute-start(bf16[4,80,1024]{2,1,0:T(8,128)(2,1)} %collective-permute-done.7.refs_2_), channel_id=1, source_target_pairs={{0,4},{1,5},{2,6},{3,7},{4,8},{5,9},{6,10},{7,11},{8,12},{9,13},{1... | collective-permute-start | bytes 1966088 | tf_op jit(solution)/shard_map/ppermute | solution.py:54
  65.7 35.1 %collective-permute-start.11 = (bf16[4,80,1024]{2,1,0:T(8,128)(2,1)}, bf16[4,80,1024]{2,1,0:T(8,128)(2,1)}, u32[]{:S(2)}, u32[]{:S(2)}) collective-permute-start(bf16[4,80,1024]{2,1,0:T(8,128)(2,1)} %collective-permute-done.10.refs_5_), channel_id=1, source_target_pairs={{0,28},{1,29},{2,30},{3,31},{4,0},{5,1},{6,2},{7,3},{8,4},{9,5},{1... | collective-permute-start | bytes 1966088 | tf_op jit(solution)/shard_map/ppermute | solution.py:54
  76.6 33.9 %collective-permute-start.15 = (bf16[8,32,1024]{2,1,0:T(8,128)(2,1)S(1)}, bf16[8,32,1024]{2,1,0:T(8,128)(2,1)}, u32[]{:S(2)}, u32[]{:S(2)}) collective-permute-start(bf16[8,32,1024]{2,1,0:T(8,128)(2,1)S(1)} %all-to-all-done.1.refs_9_), channel_id=1, source_target_pairs={{0,32},{1,33},{2,34},{3,35},{4,36},{5,37},{6,38},{7,39},{8,40},{9,... | collective-permute-start | bytes 1572872 | tf_op jit(solution)/shard_map/ppermute | solution.py:54
  76.8 33.7 %collective-permute-start.16 = (bf16[8,32,1024]{2,1,0:T(8,128)(2,1)S(1)}, bf16[8,32,1024]{2,1,0:T(8,128)(2,1)}, u32[]{:S(2)}, u32[]{:S(2)}) collective-permute-start(bf16[8,32,1024]{2,1,0:T(8,128)(2,1)S(1)} %all-to-all-done.1.refs_9_), channel_id=1, source_target_pairs={{0,34},{1,35},{2,32},{3,33},{4,38},{5,39},{6,36},{7,37},{8,42},{9,... | collective-permute-start | bytes 1572872 | tf_op jit(solution)/shard_map/ppermute | solution.py:54
  87.4 23.0 %collective-permute-start.17 = (bf16[8,32,1024]{2,1,0:T(8,128)(2,1)S(1)}, bf16[8,32,1024]{2,1,0:T(8,128)(2,1)}, u32[]{:S(2)}, u32[]{:S(2)}) collective-permute-start(bf16[8,32,1024]{2,1,0:T(8,128)(2,1)S(1)} %all-to-all-done.1.refs_9_), channel_id=1, source_target_pairs={{0,2},{1,3},{2,0},{3,1},{4,6},{5,7},{6,4},{7,5},{8,10},{9,11},{10,... | collective-permute-start | bytes 1572872 | tf_op jit(solution)/shard_map/ppermute | solution.py:54
  91.3 15.5 %all-to-all-start = ((f32[32,2,128]{2,1,0:T(2,128)}), f32[32,2,128]{2,1,0:T(2,128)S(1)}, u32[]{:S(2)}, u32[]{:S(2)}) async-start(f32[32,2,128]{2,1,0:T(2,128)} %reshape.127), calls=%async_computation | async-start | bytes 65536 | tf_op jit(solution)/shard_map/all_to_all | solution.py:224
  100.7 15.3 %collective-permute-start.12 = (bf16[4,48,1024]{2,1,0:T(8,128)(2,1)}, bf16[4,48,1024]{2,1,0:T(8,128)(2,1)}, u32[]{:S(2)}, u32[]{:S(2)}) collective-permute-start(bf16[4,48,1024]{2,1,0:T(8,128)(2,1)} %slice.200), channel_id=1, source_target_pairs={{0,4},{1,5},{2,6},{3,7},{4,8},{5,9},{6,10},{7,11},{8,12},{9,13},{1... | collective-permute-start | bytes 1179656 | tf_op jit(solution)/shard_map/ppermute | solution.py:54
  108.1 8.0 %collective-permute-start.13 = (bf16[4,32,1024]{2,1,0:T(8,128)(2,1)S(1)}, bf16[4,32,1024]{2,1,0:T(8,128)(2,1)S(1)}, u32[]{:S(2)}, u32[]{:S(2)}) collective-permute-start(bf16[4,32,1024]{2,1,0:T(8,128)(2,1)S(1)} %slice.201), channel_id=1, source_target_pairs={{0,28},{1,29},{2,30},{3,31},{4,0},{5,1},{6,2},{7,3},{8,4},{9,5},{1... | collective-permute-start | bytes 786440 | tf_op jit(solution)/shard_map/ppermute | solution.py:54
  119.3 2.7 %collective-permute-start.19 = (bf16[512,1024]{1,0:T(8,128)(2,1)S(1)}, bf16[512,1024]{1,0:T(8,128)(2,1)S(1)}, u32[]{:S(2)}, u32[]{:S(2)}) collective-permute-start(bf16[512,1024]{1,0:T(8,128)(2,1)S(1)} %get-tuple-element.20.own), channel_id=1, source_target_pairs={{0,1},{1,0},{2,3},{3,2},{4,5},{5,4},{6,7},{7,6},{8,9},{9,8},{10,11... | collective-permute-start | bytes 3145736 | tf_op jit(solution)/shard_map/ppermute | solution.py:54
  119.4 3.3 %collective-permute-start = (f32[8,1024]{1,0:T(8,128)S(1)}, f32[8,1024]{1,0:T(8,128)S(1)}, u32[]{:S(2)}, u32[]{:S(2)}) collective-permute-start(f32[8,1024]{1,0:T(8,128)S(1)} %reshape.129.refs_13_.own), channel_id=1, source_target_pairs={{0,1},{1,0},{2,3},{3,2},{4,5},{5,4},{6,7},{7,6},{8,9},{9,8},{10,11... | collective-permute-start | bytes 98312 | tf_op jit(solution)/shard_map/ppermute | solution.py:54
  125.9 4.3 %collective-permute-start.20 = (bf16[8,3584]{1,0:T(8,128)(2,1)S(1)}, bf16[8,3584]{1,0:T(8,128)(2,1)S(1)}, u32[]{:S(2)}, u32[]{:S(2)}) collective-permute-start(bf16[8,3584]{1,0:T(8,128)(2,1)S(1)} %pad_maximum_fusion.4), channel_id=1, source_target_pairs={{0,64},{1,65},{2,66},{3,67},{4,68},{5,69},{6,70},{7,71},{8,72},{9,... | collective-permute-start | bytes 172040 | tf_op jit(solution)/shard_map/ppermute | solution.py:54
  133.9 5.4 %collective-permute-start.22 = (bf16[8,3072]{1,0:T(8,128)(2,1)S(1)}, bf16[8,3072]{1,0:T(8,128)(2,1)S(1)}, u32[]{:S(2)}, u32[]{:S(2)}) collective-permute-start(bf16[8,3072]{1,0:T(8,128)(2,1)S(1)} %pad_maximum_fusion.6), channel_id=1, source_target_pairs={{0,192},{1,193},{2,194},{3,195},{4,196},{5,197},{6,198},{7,199},{8... | collective-permute-start | bytes 147464 | tf_op jit(solution)/shard_map/ppermute | solution.py:54
  143.0 4.2 %collective-permute-start.24 = (bf16[8,3072]{1,0:T(8,128)(2,1)S(1)}, bf16[8,3072]{1,0:T(8,128)(2,1)S(1)}, u32[]{:S(2)}, u32[]{:S(2)}) collective-permute-start(bf16[8,3072]{1,0:T(8,128)(2,1)S(1)} %pad_maximum_fusion.7), channel_id=1, source_target_pairs={{0,64},{1,65},{2,66},{3,67},{4,68},{5,69},{6,70},{7,71},{8,72},{9,... | collective-permute-start | bytes 147464 | tf_op jit(solution)/shard_map/ppermute | solution.py:54
  148.0 1.3 collective-permute-start.25
  154.0 4.2 %collective-permute-start.27 = (bf16[8,3072]{1,0:T(8,128)(2,1)S(1)}, bf16[8,3072]{1,0:T(8,128)(2,1)S(1)}, u32[]{:S(2)}, u32[]{:S(2)}) collective-permute-start(bf16[8,3072]{1,0:T(8,128)(2,1)S(1)} %pad_maximum_fusion.8), channel_id=1, source_target_pairs={{0,64},{1,65},{2,66},{3,67},{4,68},{5,69},{6,70},{7,71},{8,72},{9,... | collective-permute-start | bytes 147464 | tf_op jit(solution)/shard_map/ppermute | solution.py:54
  159.5 1.3 collective-permute-start.28
  161.7 5.4 %collective-permute-start.29 = (bf16[8,3072]{1,0:T(8,128)(2,1)S(1)}, bf16[8,3072]{1,0:T(8,128)(2,1)S(1)}, u32[]{:S(2)}, u32[]{:S(2)}) collective-permute-start(bf16[8,3072]{1,0:T(8,128)(2,1)S(1)} %pad_maximum_fusion.9), channel_id=1, source_target_pairs={{0,192},{1,193},{2,194},{3,195},{4,196},{5,197},{6,198},{7,199},{8... | collective-permute-start | bytes 147464 | tf_op jit(solution)/shard_map/ppermute | solution.py:54
  168.4 1.3 collective-permute-start.30
  170.7 4.3 %collective-permute-start.31 = (bf16[8,3584]{1,0:T(8,128)(2,1)S(1)}, bf16[8,3584]{1,0:T(8,128)(2,1)S(1)}, u32[]{:S(2)}, u32[]{:S(2)}) collective-permute-start(bf16[8,3584]{1,0:T(8,128)(2,1)S(1)} %pad_maximum_fusion.5), channel_id=1, source_target_pairs={{0,64},{1,65},{2,66},{3,67},{4,68},{5,69},{6,70},{7,71},{8,72},{9,... | collective-permute-start | bytes 172040 | tf_op jit(solution)/shard_map/ppermute | solution.py:54
  177.3 1.3 collective-permute-start.32
  (5 other events, 5.9 us)

commit v2 on v1

--- a/solution.py
+++ b/solution.py
@@ -186,8 +186,7 @@
     ]
     outs[1][...] = jnp.concatenate(parts, axis=1).astype(BF)
     if stage == 0:
-        for c in range(2):
-            outs[2][:, c * width : (c + 1) * width] = dot(parts[1].astype(BF), jump[c], NN)
+        jump_body(ids, parts[1].astype(BF), jump, outs[2])
 
 
 def solve(rhs, coupling, diag_inverse):
@@ -278,6 +277,7 @@
 
     solved = dot(mine_of(kept), inverse, NT)
     back = dot(solved.astype(BF), inverse, NN)
+    solved = send(solved.astype(BF), CROSS)
     other = send(back, CORE)
     back = jnp.concatenate([jnp.where(core == 0, back, other), jnp.where(core == 0, other, back)], axis=1)
 
@@ -318,9 +318,11 @@
         sent = [halves, give.astype(BF)] + ([got_x[:, :half]] if stage == 2 else [])
         arrived = send(jnp.concatenate(sent, axis=1), SWAPS[stage])
 
-    final = send(jnp.concatenate([mine_of(answer), solved], axis=1).astype(BF), CROSS)
-    solved = final[:, width:].reshape(cols, ROW, rows).transpose(1, 0, 2)
-    final = final[:, :width].reshape(cols, 2, 2, 8, rows).transpose(3, 2, 1, 0, 4).reshape(ROW, cols, rows)
+    low, high = answer[:, :width].astype(BF), answer[:, width:].astype(BF)
+    there = send(jnp.where(xl == 0, high, low), XL)
+    final = jnp.where(core == xl, jnp.where(xl == 0, low, high), there)
+    solved = solved.reshape(cols, ROW, rows).transpose(1, 0, 2)
+    final = final.reshape(cols, 2, 2, 8, rows).transpose(3, 2, 1, 0, 4).reshape(ROW, cols, rows)
     final = jnp.concatenate([final, solved], axis=1).reshape(ROW, 2 * cols * rows // 128, 128)
     got = lax.all_to_all(final, "row", 0, 0, tiled=True).astype(F32)
     got = got.reshape(ROW, 2, cols, rows).transpose(1, 3, 0, 2).reshape(2, rows, total)

time: 204 us -> 204 us (level)
  blocking collectives: 18.3 us -> 13.9 us
  starting transfers between devices: 54.9 us -> 58.2 us
    all_to_all x1, blocking collectives: 18.3 us -> 13.9 us  [solve(): got = lax.all_to_all(final, 'row', 0, 0, tiled=True).astype(F32)]
    ppermute x33 -> x34, starting transfers between devices: 39.2 us -> 42.5 us  [send(): return lax.ppermute(x, BOTH, pairs)]
    ppermute x33 -> x34, waiting for transfers between devices: 69.5 us -> 70.4 us  [send(): return lax.ppermute(x, BOTH, pairs)]
  transfers between devices with their start and end apart: 36 -> 37, of which waited for: 25 -> 26; matrix products, arithmetic and copies ran while one was open for 6% -> 6% of each run, Pallas kernels for 1% -> 2%
where the time goes in v2:
time: 204 us; the launch traced here: 201 us
  waiting for transfers between devices  81.9 us (40%)
  starting transfers between devices  58.2 us (29%)
  Pallas kernels  24.4 us (12%)
  blocking collectives  13.9 us (7%)
  matrix products  9.55 us (5%)
  local copies, waits for them, and re-layouts  9.08 us (4%)
  other arithmetic  2.26 us (1%)
    ppermute x34, waiting for transfers between devices, send(): return lax.ppermute(x, BOTH, pairs)  70.4 us
    ppermute x34, starting transfers between devices, send(): return lax.ppermute(x, BOTH, pairs)  42.5 us
    pallas_call x16, Pallas kernels, call(): pl.pallas_call(body, out_shape=out, in_specs=specs, out_specs=[pl.BlockSp...  24.4 us
    all_to_all x1, blocking collectives, solve(): got = lax.all_to_all(final, 'row', 0, 0, tiled=True).astype(F32)  13.9 us
    dot_general x10, matrix products, dot(): return lax.dot_general(a, b, dims, preferred_element_type=F32)  9.55 us
    all_to_all x1, starting transfers between devices, solve(): lax.all_to_all(lanes, BOTH, 0, 0, axis_index_groups=PLANES, tiled=True)  7.66 us
    all_to_all x1, waiting for transfers between devices, solve(): lax.all_to_all(jnp.broadcast_to(skip, (8, rows, width)), BOTH, 0, 0, axis...  6.97 us
    all_to_all x1, starting transfers between devices, solve(): lax.all_to_all(jnp.broadcast_to(skip, (8, rows, width)), BOTH, 0, 0, axis...  5.83 us
  transfers between devices with their start and end apart: 37, of which 26 were waited for; matrix products, arithmetic and copies ran while one was open for 6% of the time, Pallas kernels for 2%

profile of v2, /device:TPU:4, one launch (start us, length us, event | category | flops | bytes accessed | tf_op | source)
XLA Modules:
  0.0 200.5 jit_solution(8191388085195781451)
XLA Ops:
  2.2 2.5 %fusion.12 = bf16[256,1024]{1,0:T(8,128)(2,1)S(1)} fusion(s32[1024]{0:T(1024)S(1)} %fusion.54, bf16[256,1024]{1,0:T(8,128)(2,1)} %bitcast.90, bf16[1,1024,1024]{2,1,0:T(8,128)(2,1)S(1)} %copy-done), kind=kOutput, calls=%fused_computation.11 | convolution fusion | flops 1075314688 | bytes 3149824 | tf_op jit(solution)/shard_map/dot_general | solution.py:58
  6.0 3.1 %collective-permute-start.1 = (bf16[2,32,1024]{2,1,0:T(8,128)(2,1)S(1)}, bf16[2,32,1024]{2,1,0:T(8,128)(2,1)S(1)}, u32[]{:S(2)}, u32[]{:S(2)}) collective-permute-start(bf16[2,32,1024]{2,1,0:T(8,128)(2,1)S(1)} %bitcast.89), channel_id=1, source_target_pairs={{0,192},{1,193},{2,194},{3,195},{4,196},{5,197},{6,198},{7,199},{8... | collective-permute-start | bytes 393224 | tf_op jit(solution)/shard_map/ppermute | solution.py:54
  9.1 3.2 %collective-permute-done.1 = bf16[2,32,1024]{2,1,0:T(8,128)(2,1)S(1)} collective-permute-done((bf16[2,32,1024]{2,1,0:T(8,128)(2,1)S(1)}, bf16[2,32,1024]{2,1,0:T(8,128)(2,1)S(1)}, u32[]{:S(2)}, u32[]{:S(2)}) %collective-permute-start.1) | collective-permute-done | bytes 131104 | tf_op jit(solution)/shard_map/ppermute | solution.py:54
  16.7 2.3 %collective-permute-done.3 = bf16[80,1024]{1,0:T(8,128)(2,1)S(1)} collective-permute-done((bf16[80,1024]{1,0:T(8,128)(2,1)S(1)}, bf16[80,1024]{1,0:T(8,128)(2,1)S(1)}, u32[]{:S(2)}, u32[]{:S(2)}) %collective-permute-start.3) | collective-permute-done | bytes 163872 | tf_op jit(solution)/shard_map/ppermute | solution.py:54
  19.6 2.4 %collective-permute-done.5 = bf16[80,1024]{1,0:T(8,128)(2,1)S(1)} collective-permute-done((bf16[80,1024]{1,0:T(8,128)(2,1)S(1)}, bf16[80,1024]{1,0:T(8,128)(2,1)S(1)}, u32[]{:S(2)}, u32[]{:S(2)}) %collective-permute-start.5) | collective-permute-done | bytes 163872 | tf_op jit(solution)/shard_map/ppermute | solution.py:54
  23.4 3.8 %convert_bitcast_fusion = bf16[1024,1024]{1,0:T(8,128)(2,1)} fusion(bf16[1,1024,1024]{2,1,0:T(8,128)(2,1)S(1)} %copy-done, s32[1024]{0:T(1024)S(1)} %fusion.54), kind=kOutput, calls=%fused_computation.6 | convolution fusion | flops 2149580800 | bytes 4198400 | tf_op jit(solution)/shard_map/dot_general | solution.py:58
  29.1 4.0 %collective-permute-start.9 = (bf16[4,80,1024]{2,1,0:T(8,128)(2,1)S(1)}, bf16[4,80,1024]{2,1,0:T(8,128)(2,1)}, u32[]{:S(2)}, u32[]{:S(2)}) collective-permute-start(bf16[4,80,1024]{2,1,0:T(8,128)(2,1)S(1)} %pad_maximum_fusion.refs_0_), channel_id=1, source_target_pairs={{0,28},{1,29},{2,30},{3,31},{4,0},{5,1},{6,2},{7,3},{8,4},{9,5},{1... | collective-permute-start | bytes 1966088 | tf_op jit(solution)/shard_map/ppermute | solution.py:54
  33.1 6.7 %collective-permute-done.6.refs_1_ = bf16[4,80,1024]{2,1,0:T(8,128)(2,1)} collective-permute-done((bf16[4,80,1024]{2,1,0:T(8,128)(2,1)S(1)}, bf16[4,80,1024]{2,1,0:T(8,128)(2,1)}, u32[]{:S(2)}, u32[]{:S(2)}) %collective-permute-start.6) | collective-permute-done | bytes 655392 | tf_op jit(solution)/shard_map/ppermute | solution.py:54
  42.0 4.6 %collective-permute-done.9.refs_4_ = bf16[4,80,1024]{2,1,0:T(8,128)(2,1)} collective-permute-done((bf16[4,80,1024]{2,1,0:T(8,128)(2,1)S(1)}, bf16[4,80,1024]{2,1,0:T(8,128)(2,1)}, u32[]{:S(2)}, u32[]{:S(2)}) %collective-permute-start.9) | collective-permute-done | bytes 655392 | tf_op jit(solution)/shard_map/ppermute | solution.py:54
  46.7 3.8 %collective-permute-start.10 = (bf16[4,80,1024]{2,1,0:T(8,128)(2,1)}, bf16[4,80,1024]{2,1,0:T(8,128)(2,1)}, u32[]{:S(2)}, u32[]{:S(2)}) collective-permute-start(bf16[4,80,1024]{2,1,0:T(8,128)(2,1)} %collective-permute-done.9.refs_4_), channel_id=1, source_target_pairs={{0,28},{1,29},{2,30},{3,31},{4,0},{5,1},{6,2},{7,3},{8,4},{9,5},{1... | collective-permute-start | bytes 1966088 | tf_op jit(solution)/shard_map/ppermute | solution.py:54
  51.4 5.8 %all-to-all-start.1 = ((bf16[8,32,1024]{2,1,0:T(8,128)(2,1)}), bf16[8,32,1024]{2,1,0:T(8,128)(2,1)S(1)}, u32[]{:S(2)}, u32[]{:S(2)}) async-start(bf16[8,32,1024]{2,1,0:T(8,128)(2,1)} %broadcast_in_dim.5), calls=%async_computation.1 | async-start | bytes 1048576 | tf_op jit(solution)/shard_map/all_to_all | solution.py:228
  59.2 6.4 %collective-permute-done.10.refs_5_ = bf16[4,80,1024]{2,1,0:T(8,128)(2,1)} collective-permute-done((bf16[4,80,1024]{2,1,0:T(8,128)(2,1)}, bf16[4,80,1024]{2,1,0:T(8,128)(2,1)}, u32[]{:S(2)}, u32[]{:S(2)}) %collective-permute-start.10) | collective-permute-done | bytes 655392 | tf_op jit(solution)/shard_map/ppermute | solution.py:54
  65.7 3.9 %collective-permute-start.11 = (bf16[4,80,1024]{2,1,0:T(8,128)(2,1)}, bf16[4,80,1024]{2,1,0:T(8,128)(2,1)}, u32[]{:S(2)}, u32[]{:S(2)}) collective-permute-start(bf16[4,80,1024]{2,1,0:T(8,128)(2,1)} %collective-permute-done.10.refs_5_), channel_id=1, source_target_pairs={{0,28},{1,29},{2,30},{3,31},{4,0},{5,1},{6,2},{7,3},{8,4},{9,5},{1... | collective-permute-start | bytes 1966088 | tf_op jit(solution)/shard_map/ppermute | solution.py:54
  69.6 7.0 %all-to-all-done.1.refs_9_ = bf16[8,32,1024]{2,1,0:T(8,128)(2,1)S(1)} async-done(((bf16[8,32,1024]{2,1,0:T(8,128)(2,1)}), bf16[8,32,1024]{2,1,0:T(8,128)(2,1)S(1)}, u32[]{:S(2)}, u32[]{:S(2)}) %all-to-all-start.1) | async-done | bytes 524320 | tf_op jit(solution)/shard_map/all_to_all | solution.py:228
  78.6 8.8 %collective-permute-done.8.refs_3_ = bf16[4,80,1024]{2,1,0:T(8,128)(2,1)} collective-permute-done((bf16[4,80,1024]{2,1,0:T(8,128)(2,1)}, bf16[4,80,1024]{2,1,0:T(8,128)(2,1)}, u32[]{:S(2)}, u32[]{:S(2)}) %collective-permute-start.8) | collective-permute-done | bytes 655392 | tf_op jit(solution)/shard_map/ppermute | solution.py:54
  91.3 7.7 %all-to-all-start = ((f32[32,2,128]{2,1,0:T(2,128)}), f32[32,2,128]{2,1,0:T(2,128)S(1)}, u32[]{:S(2)}, u32[]{:S(2)}) async-start(f32[32,2,128]{2,1,0:T(2,128)} %reshape.127), calls=%async_computation | async-start | bytes 65536 | tf_op jit(solution)/shard_map/all_to_all | solution.py:223
  102.3 4.5 %all-to-all-done = f32[32,2,128]{2,1,0:T(2,128)S(1)} async-done(((f32[32,2,128]{2,1,0:T(2,128)}), f32[32,2,128]{2,1,0:T(2,128)S(1)}, u32[]{:S(2)}, u32[]{:S(2)}) %all-to-all-start) | async-done | bytes 32800 | tf_op jit(solution)/shard_map/all_to_all | solution.py:223
  110.5 5.5 %collective-permute-done.13.refs_8_ = bf16[4,32,1024]{2,1,0:T(8,128)(2,1)S(1)} collective-permute-done((bf16[4,32,1024]{2,1,0:T(8,128)(2,1)S(1)}, bf16[4,32,1024]{2,1,0:T(8,128)(2,1)S(1)}, u32[]{:S(2)}, u32[]{:S(2)}) %collective-permute-start.13) | collective-permute-done | bytes 262176 | tf_op jit(solution)/shard_map/ppermute | solution.py:54
  116.0 3.2 %shard_map.50 = (bf16[2,2,512,1024]{3,2,1,0:T(8,128)(2,1)S(1)}, bf16[2,512,1024]{2,1,0:T(8,128)(2,1)S(1)}, bf16[512,1024]{1,0:T(8,128)(2,1)S(1)}) custom-call(s32[5]{0:T(128)S(1)} %stack.38.ids, bf16[4,80,1024]{2,1,0:T(8,128)(2,1)S(1)} %pad_maximum_fusion.refs_0_, bf16[4,80,1024]{2,1,0:T(8,128)(2,1)} %collective-permute-done.6.refs_1_, ...), custom_call_target="tpu_custom_call" | custom-call | tf_op jit(solution)/shard_map/pallas_call | solution.py:65
  122.7 3.1 %shard_map.52 = (bf16[8,2048]{1,0:T(8,128)(2,1)S(1)}, f32[8,1536]{1,0:T(8,128)S(1)}) custom-call(s32[5]{0:T(128)S(1)} %stack.38.ids, f32[8,1024]{1,0:T(8,128)S(1)} %reshape.129.refs_13_.own, f32[8,1024]{1,0:T(8,128)S(1)} %collective-permute-done.other, bf16[8,2048]{1,0:T(8,128)(2,1)S(1)} %broadcast_5_old_near_from_own_other.2.old.near_from.own.other, ...), custom_call_target="tpu_custom_call" | custom-call | tf_op jit(solution)/shard_map/pallas_call | solution.py:65
  126.0 4.2 %collective-permute-done.20 = bf16[8,3584]{1,0:T(8,128)(2,1)S(1)} collective-permute-done((bf16[8,3584]{1,0:T(8,128)(2,1)S(1)}, bf16[8,3584]{1,0:T(8,128)(2,1)S(1)}, u32[]{:S(2)}, u32[]{:S(2)}) %collective-permute-start.20) | collective-permute-done | bytes 57376 | tf_op jit(solution)/shard_map/ppermute | solution.py:54
  131.4 2.5 %shard_map.53 = (bf16[8,2048]{1,0:T(8,128)(2,1)S(1)}, f32[8,1024]{1,0:T(8,128)S(1)}) custom-call(s32[5]{0:T(128)S(1)} %stack.38.ids, f32[8,1024]{1,0:T(8,128)S(1)} %convert_subtract_fusion.1.own, f32[8,1024]{1,0:T(8,128)S(1)} %collective-permute-done.21.other, bf16[8,2048]{1,0:T(8,128)(2,1)S(1)} %get-tuple-element.22.old, ...), custom_call_target="tpu_custom_call" | custom-call | tf_op jit(solution)/shard_map/pallas_call | solution.py:65
  133.9 2.6 %collective-permute-start.22 = (bf16[8,3072]{1,0:T(8,128)(2,1)S(1)}, bf16[8,3072]{1,0:T(8,128)(2,1)S(1)}, u32[]{:S(2)}, u32[]{:S(2)}) collective-permute-start(bf16[8,3072]{1,0:T(8,128)(2,1)S(1)} %pad_maximum_fusion.6), channel_id=1, source_target_pairs={{0,192},{1,193},{2,194},{3,195},{4,196},{5,197},{6,198},{7,199},{8... | collective-permute-start | bytes 147464 | tf_op jit(solution)/shard_map/ppermute | solution.py:54
  136.5 2.8 %collective-permute-done.22 = bf16[8,3072]{1,0:T(8,128)(2,1)S(1)} collective-permute-done((bf16[8,3072]{1,0:T(8,128)(2,1)S(1)}, bf16[8,3072]{1,0:T(8,128)(2,1)S(1)}, u32[]{:S(2)}, u32[]{:S(2)}) %collective-permute-start.22) | collective-permute-done | bytes 49184 | tf_op jit(solution)/shard_map/ppermute | solution.py:54
  140.5 2.5 %shard_map.54 = (bf16[8,2048]{1,0:T(8,128)(2,1)S(1)}, f32[8,1024]{1,0:T(8,128)S(1)}) custom-call(s32[5]{0:T(128)S(1)} %stack.38.ids, f32[8,1024]{1,0:T(8,128)S(1)} %convert_subtract_fusion.own, f32[8,1024]{1,0:T(8,128)S(1)} %collective-permute-done.23.other, bf16[8,2048]{1,0:T(8,128)(2,1)S(1)} %get-tuple-element.24.old, ...), custom_call_target="tpu_custom_call" | custom-call | tf_op jit(solution)/shard_map/pallas_call | solution.py:65
  143.1 4.1 %collective-permute-done.24 = bf16[8,3072]{1,0:T(8,128)(2,1)S(1)} collective-permute-done((bf16[8,3072]{1,0:T(8,128)(2,1)S(1)}, bf16[8,3072]{1,0:T(8,128)(2,1)S(1)}, u32[]{:S(2)}, u32[]{:S(2)}) %collective-permute-start.24) | collective-permute-done | bytes 49184 | tf_op jit(solution)/shard_map/ppermute | solution.py:54
  154.3 4.1 %collective-permute-done.27 = bf16[8,3072]{1,0:T(8,128)(2,1)S(1)} collective-permute-done((bf16[8,3072]{1,0:T(8,128)(2,1)S(1)}, bf16[8,3072]{1,0:T(8,128)(2,1)S(1)}, u32[]{:S(2)}, u32[]{:S(2)}) %collective-permute-start.27) | collective-permute-done | bytes 49184 | tf_op jit(solution)/shard_map/ppermute | solution.py:54
  161.9 2.6 %collective-permute-start.29 = (bf16[8,3072]{1,0:T(8,128)(2,1)S(1)}, bf16[8,3072]{1,0:T(8,128)(2,1)S(1)}, u32[]{:S(2)}, u32[]{:S(2)}) collective-permute-start(bf16[8,3072]{1,0:T(8,128)(2,1)S(1)} %pad_maximum_fusion.9), channel_id=1, source_target_pairs={{0,192},{1,193},{2,194},{3,195},{4,196},{5,197},{6,198},{7,199},{8... | collective-permute-start | bytes 147464 | tf_op jit(solution)/shard_map/ppermute | solution.py:54
  164.5 2.8 %collective-permute-done.29 = bf16[8,3072]{1,0:T(8,128)(2,1)S(1)} collective-permute-done((bf16[8,3072]{1,0:T(8,128)(2,1)S(1)}, bf16[8,3072]{1,0:T(8,128)(2,1)S(1)}, u32[]{:S(2)}, u32[]{:S(2)}) %collective-permute-start.29) | collective-permute-done | bytes 49184 | tf_op jit(solution)/shard_map/ppermute | solution.py:54
  171.0 4.2 %collective-permute-done.31 = bf16[8,3584]{1,0:T(8,128)(2,1)S(1)} collective-permute-done((bf16[8,3584]{1,0:T(8,128)(2,1)S(1)}, bf16[8,3584]{1,0:T(8,128)(2,1)S(1)}, u32[]{:S(2)}, u32[]{:S(2)}) %collective-permute-start.31) | collective-permute-done | bytes 57376 | tf_op jit(solution)/shard_map/ppermute | solution.py:54
  179.8 3.3 %collective-permute-start.33 = (bf16[8,1024]{1,0:T(8,128)(2,1)S(1)}, bf16[8,1024]{1,0:T(8,128)(2,1)S(1)}, u32[]{:S(2)}, u32[]{:S(2)}) collective-permute-start(bf16[8,1024]{1,0:T(8,128)(2,1)S(1)} %broadcast_select_fusion.3), channel_id=1, source_target_pairs={{0,32},{1,33},{2,34},{3,35},{4,36},{5,37},{6,38},{7,39},{8,40},{9,... | collective-permute-start | bytes 49160 | tf_op jit(solution)/shard_map/ppermute | solution.py:54
  185.1 13.9 %all_to_all.15 = bf16[32,4,128]{2,1,0:T(4,128)(2,1)S(1)} all-to-all(bf16[32,4,128]{2,1,0:T(4,128)(2,1)S(1)} %reshape.136), channel_id=1, replica_groups=mesh['sec'=8,'row'=32] {'row'}, dimensions={0} | all-to-all | bytes 65536 | tf_op jit(solution)/shard_map/all_to_all | solution.py:327
  (137 shorter events, 57.5 us)
Async XLA Ops:
  4.7 4.4 %collective-permute-start.2 = (bf16[16,1024]{1,0:T(8,128)(2,1)S(1)}, bf16[16,1024]{1,0:T(8,128)(2,1)S(1)}, u32[]{:S(2)}, u32[]{:S(2)}) collective-permute-start(bf16[16,1024]{1,0:T(8,128)(2,1)S(1)} %dynamic-slice_bitcast_fusion), channel_id=1, source_target_pairs={{0,32},{1,33},{2,34},{3,35},{4,36},{5,37},{6,38},{7,39},{8,40},{9,... | collective-permute-start | bytes 98312 | tf_op jit(solution)/shard_map/ppermute | solution.py:54
  6.0 6.3 %collective-permute-start.1 = (bf16[2,32,1024]{2,1,0:T(8,128)(2,1)S(1)}, bf16[2,32,1024]{2,1,0:T(8,128)(2,1)S(1)}, u32[]{:S(2)}, u32[]{:S(2)}) collective-permute-start(bf16[2,32,1024]{2,1,0:T(8,128)(2,1)S(1)} %bitcast.89), channel_id=1, source_target_pairs={{0,192},{1,193},{2,194},{3,195},{4,196},{5,197},{6,198},{7,199},{8... | collective-permute-start | bytes 393224 | tf_op jit(solution)/shard_map/ppermute | solution.py:54
  12.4 6.6 %collective-permute-start.3 = (bf16[80,1024]{1,0:T(8,128)(2,1)S(1)}, bf16[80,1024]{1,0:T(8,128)(2,1)S(1)}, u32[]{:S(2)}, u32[]{:S(2)}) collective-permute-start(bf16[80,1024]{1,0:T(8,128)(2,1)S(1)} %get-tuple-element.39), channel_id=1, source_target_pairs={{0,32},{1,33},{2,34},{3,35},{4,36},{5,37},{6,38},{7,39},{8,40},{9,... | collective-permute-start | bytes 491528 | tf_op jit(solution)/shard_map/ppermute | solution.py:54
  13.3 6.3 %collective-permute-start.4 = (bf16[80,1024]{1,0:T(8,128)(2,1)S(1)}, bf16[80,1024]{1,0:T(8,128)(2,1)S(1)}, u32[]{:S(2)}, u32[]{:S(2)}) collective-permute-start(bf16[80,1024]{1,0:T(8,128)(2,1)S(1)} %get-tuple-element.39), channel_id=1, source_target_pairs={{0,34},{1,35},{2,32},{3,33},{4,38},{5,39},{6,36},{7,37},{8,42},{9,... | collective-permute-start | bytes 491528 | tf_op jit(solution)/shard_map/ppermute | solution.py:54
  14.5 7.6 %collective-permute-start.5 = (bf16[80,1024]{1,0:T(8,128)(2,1)S(1)}, bf16[80,1024]{1,0:T(8,128)(2,1)S(1)}, u32[]{:S(2)}, u32[]{:S(2)}) collective-permute-start(bf16[80,1024]{1,0:T(8,128)(2,1)S(1)} %get-tuple-element.39), channel_id=1, source_target_pairs={{0,2},{1,3},{2,0},{3,1},{4,6},{5,7},{6,4},{7,5},{8,10},{9,11},{10,... | collective-permute-start | bytes 491528 | tf_op jit(solution)/shard_map/ppermute | solution.py:54
  22.1 17.6 %collective-permute-start.6 = (bf16[4,80,1024]{2,1,0:T(8,128)(2,1)S(1)}, bf16[4,80,1024]{2,1,0:T(8,128)(2,1)}, u32[]{:S(2)}, u32[]{:S(2)}) collective-permute-start(bf16[4,80,1024]{2,1,0:T(8,128)(2,1)S(1)} %pad_maximum_fusion.refs_0_), channel_id=1, source_target_pairs={{0,4},{1,5},{2,6},{3,7},{4,8},{5,9},{6,10},{7,11},{8,12},{9,13},{1... | collective-permute-start | bytes 1966088 | tf_op jit(solution)/shard_map/ppermute | solution.py:54
  27.2 80.9 %collective-permute-start.18 = (bf16[1024,1024]{1,0:T(8,128)(2,1)}, bf16[1024,1024]{1,0:T(8,128)(2,1)}, u32[]{:S(2)}, u32[]{:S(2)}) collective-permute-start(bf16[1024,1024]{1,0:T(8,128)(2,1)} %convert_bitcast_fusion), channel_id=1, source_target_pairs={{1,32},{3,34},{5,36},{7,38},{9,40},{11,42},{13,44},{15,46},{17,48}... | collective-permute-start | bytes 6291464 | tf_op jit(solution)/shard_map/ppermute | solution.py:54
  29.1 17.5 %collective-permute-start.9 = (bf16[4,80,1024]{2,1,0:T(8,128)(2,1)S(1)}, bf16[4,80,1024]{2,1,0:T(8,128)(2,1)}, u32[]{:S(2)}, u32[]{:S(2)}) collective-permute-start(bf16[4,80,1024]{2,1,0:T(8,128)(2,1)S(1)} %pad_maximum_fusion.refs_0_), channel_id=1, source_target_pairs={{0,28},{1,29},{2,30},{3,31},{4,0},{5,1},{6,2},{7,3},{8,4},{9,5},{1... | collective-permute-start | bytes 1966088 | tf_op jit(solution)/shard_map/ppermute | solution.py:54
  39.8 17.4 %collective-permute-start.7 = (bf16[4,80,1024]{2,1,0:T(8,128)(2,1)}, bf16[4,80,1024]{2,1,0:T(8,128)(2,1)}, u32[]{:S(2)}, u32[]{:S(2)}) collective-permute-start(bf16[4,80,1024]{2,1,0:T(8,128)(2,1)} %collective-permute-done.6.refs_1_), channel_id=1, source_target_pairs={{0,4},{1,5},{2,6},{3,7},{4,8},{5,9},{6,10},{7,11},{8,12},{9,13},{1... | collective-permute-start | bytes 1966088 | tf_op jit(solution)/shard_map/ppermute | solution.py:54
  39.8 10.7 %collective-permute-start.14 = (bf16[1,32,1024]{2,1,0:T(8,128)(2,1)S(1)}, bf16[1,32,1024]{2,1,0:T(8,128)(2,1)S(1)}, u32[]{:S(2)}, u32[]{:S(2)}) collective-permute-start(bf16[1,32,1024]{2,1,0:T(8,128)(2,1)S(1)} %constant_dynamic-slice_fusion), channel_id=1, source_target_pairs={{0,64},{32,96},{64,192},{96,224},{1,65},{33,97},{65,193},{97,225},... | collective-permute-start | bytes 196616 | tf_op jit(solution)/shard_map/ppermute | solution.py:217
  46.7 19.0 %collective-permute-start.10 = (bf16[4,80,1024]{2,1,0:T(8,128)(2,1)}, bf16[4,80,1024]{2,1,0:T(8,128)(2,1)}, u32[]{:S(2)}, u32[]{:S(2)}) collective-permute-start(bf16[4,80,1024]{2,1,0:T(8,128)(2,1)} %collective-permute-done.9.refs_4_), channel_id=1, source_target_pairs={{0,28},{1,29},{2,30},{3,31},{4,0},{5,1},{6,2},{7,3},{8,4},{9,5},{1... | collective-permute-start | bytes 1966088 | tf_op jit(solution)/shard_map/ppermute | solution.py:54
  51.4 25.2 %all-to-all-start.1 = ((bf16[8,32,1024]{2,1,0:T(8,128)(2,1)}), bf16[8,32,1024]{2,1,0:T(8,128)(2,1)S(1)}, u32[]{:S(2)}, u32[]{:S(2)}) async-start(bf16[8,32,1024]{2,1,0:T(8,128)(2,1)} %broadcast_in_dim.5), calls=%async_computation.1 | async-start | bytes 1048576 | tf_op jit(solution)/shard_map/all_to_all | solution.py:228
  57.2 30.2 %collective-permute-start.8 = (bf16[4,80,1024]{2,1,0:T(8,128)(2,1)}, bf16[4,80,1024]{2,1,0:T(8,128)(2,1)}, u32[]{:S(2)}, u32[]{:S(2)}) collective-permute-start(bf16[4,80,1024]{2,1,0:T(8,128)(2,1)} %collective-permute-done.7.refs_2_), channel_id=1, source_target_pairs={{0,4},{1,5},{2,6},{3,7},{4,8},{5,9},{6,10},{7,11},{8,12},{9,13},{1... | collective-permute-start | bytes 1966088 | tf_op jit(solution)/shard_map/ppermute | solution.py:54
  65.7 35.1 %collective-permute-start.11 = (bf16[4,80,1024]{2,1,0:T(8,128)(2,1)}, bf16[4,80,1024]{2,1,0:T(8,128)(2,1)}, u32[]{:S(2)}, u32[]{:S(2)}) collective-permute-start(bf16[4,80,1024]{2,1,0:T(8,128)(2,1)} %collective-permute-done.10.refs_5_), channel_id=1, source_target_pairs={{0,28},{1,29},{2,30},{3,31},{4,0},{5,1},{6,2},{7,3},{8,4},{9,5},{1... | collective-permute-start | bytes 1966088 | tf_op jit(solution)/shard_map/ppermute | solution.py:54
  76.6 33.9 %collective-permute-start.15 = (bf16[8,32,1024]{2,1,0:T(8,128)(2,1)S(1)}, bf16[8,32,1024]{2,1,0:T(8,128)(2,1)}, u32[]{:S(2)}, u32[]{:S(2)}) collective-permute-start(bf16[8,32,1024]{2,1,0:T(8,128)(2,1)S(1)} %all-to-all-done.1.refs_9_), channel_id=1, source_target_pairs={{0,32},{1,33},{2,34},{3,35},{4,36},{5,37},{6,38},{7,39},{8,40},{9,... | collective-permute-start | bytes 1572872 | tf_op jit(solution)/shard_map/ppermute | solution.py:54
  76.8 33.7 %collective-permute-start.16 = (bf16[8,32,1024]{2,1,0:T(8,128)(2,1)S(1)}, bf16[8,32,1024]{2,1,0:T(8,128)(2,1)}, u32[]{:S(2)}, u32[]{:S(2)}) collective-permute-start(bf16[8,32,1024]{2,1,0:T(8,128)(2,1)S(1)} %all-to-all-done.1.refs_9_), channel_id=1, source_target_pairs={{0,34},{1,35},{2,32},{3,33},{4,38},{5,39},{6,36},{7,37},{8,42},{9,... | collective-permute-start | bytes 1572872 | tf_op jit(solution)/shard_map/ppermute | solution.py:54
  87.4 23.0 %collective-permute-start.17 = (bf16[8,32,1024]{2,1,0:T(8,128)(2,1)S(1)}, bf16[8,32,1024]{2,1,0:T(8,128)(2,1)}, u32[]{:S(2)}, u32[]{:S(2)}) collective-permute-start(bf16[8,32,1024]{2,1,0:T(8,128)(2,1)S(1)} %all-to-all-done.1.refs_9_), channel_id=1, source_target_pairs={{0,2},{1,3},{2,0},{3,1},{4,6},{5,7},{6,4},{7,5},{8,10},{9,11},{10,... | collective-permute-start | bytes 1572872 | tf_op jit(solution)/shard_map/ppermute | solution.py:54
  91.3 15.5 %all-to-all-start = ((f32[32,2,128]{2,1,0:T(2,128)}), f32[32,2,128]{2,1,0:T(2,128)S(1)}, u32[]{:S(2)}, u32[]{:S(2)}) async-start(f32[32,2,128]{2,1,0:T(2,128)} %reshape.127), calls=%async_computation | async-start | bytes 65536 | tf_op jit(solution)/shard_map/all_to_all | solution.py:223
  100.7 15.3 %collective-permute-start.12 = (bf16[4,48,1024]{2,1,0:T(8,128)(2,1)}, bf16[4,48,1024]{2,1,0:T(8,128)(2,1)}, u32[]{:S(2)}, u32[]{:S(2)}) collective-permute-start(bf16[4,48,1024]{2,1,0:T(8,128)(2,1)} %slice.194), channel_id=1, source_target_pairs={{0,4},{1,5},{2,6},{3,7},{4,8},{5,9},{6,10},{7,11},{8,12},{9,13},{1... | collective-permute-start | bytes 1179656 | tf_op jit(solution)/shard_map/ppermute | solution.py:54
  108.1 8.0 %collective-permute-start.13 = (bf16[4,32,1024]{2,1,0:T(8,128)(2,1)S(1)}, bf16[4,32,1024]{2,1,0:T(8,128)(2,1)S(1)}, u32[]{:S(2)}, u32[]{:S(2)}) collective-permute-start(bf16[4,32,1024]{2,1,0:T(8,128)(2,1)S(1)} %slice.195), channel_id=1, source_target_pairs={{0,28},{1,29},{2,30},{3,31},{4,0},{5,1},{6,2},{7,3},{8,4},{9,5},{1... | collective-permute-start | bytes 786440 | tf_op jit(solution)/shard_map/ppermute | solution.py:54
  119.3 2.7 %collective-permute-start.19 = (bf16[512,1024]{1,0:T(8,128)(2,1)S(1)}, bf16[512,1024]{1,0:T(8,128)(2,1)S(1)}, u32[]{:S(2)}, u32[]{:S(2)}) collective-permute-start(bf16[512,1024]{1,0:T(8,128)(2,1)S(1)} %get-tuple-element.20.own), channel_id=1, source_target_pairs={{0,1},{1,0},{2,3},{3,2},{4,5},{5,4},{6,7},{7,6},{8,9},{9,8},{10,11... | collective-permute-start | bytes 3145736 | tf_op jit(solution)/shard_map/ppermute | solution.py:54
  119.4 3.3 %collective-permute-start = (f32[8,1024]{1,0:T(8,128)S(1)}, f32[8,1024]{1,0:T(8,128)S(1)}, u32[]{:S(2)}, u32[]{:S(2)}) collective-permute-start(f32[8,1024]{1,0:T(8,128)S(1)} %reshape.129.refs_13_.own), channel_id=1, source_target_pairs={{0,1},{1,0},{2,3},{3,2},{4,5},{5,4},{6,7},{7,6},{8,9},{9,8},{10,11... | collective-permute-start | bytes 98312 | tf_op jit(solution)/shard_map/ppermute | solution.py:54
  125.9 4.3 %collective-permute-start.20 = (bf16[8,3584]{1,0:T(8,128)(2,1)S(1)}, bf16[8,3584]{1,0:T(8,128)(2,1)S(1)}, u32[]{:S(2)}, u32[]{:S(2)}) collective-permute-start(bf16[8,3584]{1,0:T(8,128)(2,1)S(1)} %pad_maximum_fusion.4), channel_id=1, source_target_pairs={{0,64},{1,65},{2,66},{3,67},{4,68},{5,69},{6,70},{7,71},{8,72},{9,... | collective-permute-start | bytes 172040 | tf_op jit(solution)/shard_map/ppermute | solution.py:54
  133.9 5.4 %collective-permute-start.22 = (bf16[8,3072]{1,0:T(8,128)(2,1)S(1)}, bf16[8,3072]{1,0:T(8,128)(2,1)S(1)}, u32[]{:S(2)}, u32[]{:S(2)}) collective-permute-start(bf16[8,3072]{1,0:T(8,128)(2,1)S(1)} %pad_maximum_fusion.6), channel_id=1, source_target_pairs={{0,192},{1,193},{2,194},{3,195},{4,196},{5,197},{6,198},{7,199},{8... | collective-permute-start | bytes 147464 | tf_op jit(solution)/shard_map/ppermute | solution.py:54
  143.0 4.2 %collective-permute-start.24 = (bf16[8,3072]{1,0:T(8,128)(2,1)S(1)}, bf16[8,3072]{1,0:T(8,128)(2,1)S(1)}, u32[]{:S(2)}, u32[]{:S(2)}) collective-permute-start(bf16[8,3072]{1,0:T(8,128)(2,1)S(1)} %pad_maximum_fusion.7), channel_id=1, source_target_pairs={{0,64},{1,65},{2,66},{3,67},{4,68},{5,69},{6,70},{7,71},{8,72},{9,... | collective-permute-start | bytes 147464 | tf_op jit(solution)/shard_map/ppermute | solution.py:54
  148.0 1.3 collective-permute-start.25
  154.2 4.2 %collective-permute-start.27 = (bf16[8,3072]{1,0:T(8,128)(2,1)S(1)}, bf16[8,3072]{1,0:T(8,128)(2,1)S(1)}, u32[]{:S(2)}, u32[]{:S(2)}) collective-permute-start(bf16[8,3072]{1,0:T(8,128)(2,1)S(1)} %pad_maximum_fusion.8), channel_id=1, source_target_pairs={{0,64},{1,65},{2,66},{3,67},{4,68},{5,69},{6,70},{7,71},{8,72},{9,... | collective-permute-start | bytes 147464 | tf_op jit(solution)/shard_map/ppermute | solution.py:54
  161.9 5.4 %collective-permute-start.29 = (bf16[8,3072]{1,0:T(8,128)(2,1)S(1)}, bf16[8,3072]{1,0:T(8,128)(2,1)S(1)}, u32[]{:S(2)}, u32[]{:S(2)}) collective-permute-start(bf16[8,3072]{1,0:T(8,128)(2,1)S(1)} %pad_maximum_fusion.9), channel_id=1, source_target_pairs={{0,192},{1,193},{2,194},{3,195},{4,196},{5,197},{6,198},{7,199},{8... | collective-permute-start | bytes 147464 | tf_op jit(solution)/shard_map/ppermute | solution.py:54
  168.7 1.3 collective-permute-start.30
  170.9 4.3 %collective-permute-start.31 = (bf16[8,3584]{1,0:T(8,128)(2,1)S(1)}, bf16[8,3584]{1,0:T(8,128)(2,1)S(1)}, u32[]{:S(2)}, u32[]{:S(2)}) collective-permute-start(bf16[8,3584]{1,0:T(8,128)(2,1)S(1)} %pad_maximum_fusion.5), channel_id=1, source_target_pairs={{0,64},{1,65},{2,66},{3,67},{4,68},{5,69},{6,70},{7,71},{8,72},{9,... | collective-permute-start | bytes 172040 | tf_op jit(solution)/shard_map/ppermute | solution.py:54
  177.7 5.4 %collective-permute-start.34 = (bf16[8,1024]{1,0:T(8,128)(2,1)S(1)}, bf16[8,1024]{1,0:T(8,128)(2,1)S(1)}, u32[]{:S(2)}, u32[]{:S(2)}) collective-permute-start(bf16[8,1024]{1,0:T(8,128)(2,1)S(1)} %convolution_convert_fusion), channel_id=1, source_target_pairs={{0,0},{1,32},{2,2},{3,34},{4,4},{5,36},{6,6},{7,38},{8,8},{9,40},{... | collective-permute-start | bytes 49160 | tf_op jit(solution)/shard_map/ppermute | solution.py:54
  179.8 5.0 %collective-permute-start.33 = (bf16[8,1024]{1,0:T(8,128)(2,1)S(1)}, bf16[8,1024]{1,0:T(8,128)(2,1)S(1)}, u32[]{:S(2)}, u32[]{:S(2)}) collective-permute-start(bf16[8,1024]{1,0:T(8,128)(2,1)S(1)} %broadcast_select_fusion.3), channel_id=1, source_target_pairs={{0,32},{1,33},{2,34},{3,35},{4,36},{5,37},{6,38},{7,39},{8,40},{9,... | collective-permute-start | bytes 49160 | tf_op jit(solution)/shard_map/ppermute | solution.py:54
  (6 other events, 7.8 us)
